TPU v7x, 32 devices: a whole 2x2x4 slice. The times are simulated.
32 devices in a mesh: row: 8 (over z, x), col: 2 (over y), rep: 2 (over core).
Axes of the slice: x: 2, y: 2, z: 4, core: 2. Of those that a mesh axis runs over, the one named last changes fastest.
Arguments:
- matrix: float32 [16384, 16384], P('row', 'col'), may hold values from -0.125 to 0.125
- vectors: float32 [64, 16384], P('rep', 'row'), may hold values from -0.3 to 0.3
Outputs:
- result: float32 [64, 16384], P('rep', 'row')
All inputs are finite; a program needn't handle non-finite values.
Results may differ from a plain program's by a relative error of at most 0.00011.
Values sent between devices are 32-bit elements; how exact they have to be, the bound alone decides.
No kernel may reach another device: no remote copies, remote signals or barrier semaphores. Data moves between devices by JAX's collectives and lax.ppermute only.
A program may use at most 128 MiB of HBM per device.

v0:
```python
import jax
import jax.numpy as jnp
from jax import lax
from jax.sharding import PartitionSpec as P

TERMS = 6
STEPS = 1


def broadcast(block, axis, holder):
    block = jnp.where(lax.axis_index(axis) == holder, block, jnp.zeros_like(block))
    return lax.psum(block, axis)


def apply_matrix(current, matrix):
    fanout = lax.axis_size("row") // lax.axis_size("col")
    column_index = lax.axis_index("col")
    pieces = [broadcast(current, "row", column_index * fanout + which) for which in range(fanout)]
    operand = jnp.concatenate(pieces, axis=1)
    partial_value = lax.dot_general(
        operand,
        matrix,
        (((1,), (1,)), ((), ())),
        precision=lax.Precision.HIGHEST,
        preferred_element_type=jnp.float32,
    )
    return lax.psum(partial_value, "col")


def local(matrix, vectors):
    summand = vectors
    running = vectors
    for degree in range(1, TERMS + 1):
        summand = apply_matrix(summand, matrix) / float(degree * STEPS)
        running = running + summand
    return running


def solution(mesh):
    placed = (P("row", "col"), P("rep", "row"))
    return jax.shard_map(
        local, mesh=mesh, in_specs=placed, out_specs=P("rep", "row"), check_vma=False
    )
```

profile of v0, /device:TPU:0, one launch (start us, length us, event | category | flops | bytes accessed | tf_op | source)
XLA Modules:
  0.0 1029.5 jit_solution(9411824174395434742)
XLA Ops:
  6.5 0.0 all-reduce.41.cloned.1.call-start
  6.5 1.9 broadcast_select_fusion.7
  8.5 0.0 all-reduce.41.cloned.1.call-update
  8.5 0.0 all-reduce.19.cloned.1.call-start
  8.6 83.8 %all-reduce.41.cloned.1.call-done = (f32[32,2048]{1,0:T(8,128)}, f32[32,2048]{1,0:T(8,128)}, f32[32,2048]{1,0:T(8,128)}, f32[32,2048]{1,0:T(8,128)}) async-done(((f32[32,2048]{1,0:T(8,128)}, f32[32,2048]{1,0:T(8,128)}, f32[32,2048]{1,0:T(8,128)}, f32[32,2048]{1,0:T(8,128)}), (f32[32,2048]{1,0:T(8,128)}, f32[32,2048]{1,0:T(8,128)}, f32[32,2048]{1,0:T(8,128)}, ...) | async-done | bytes 1048592 | tf_op jit(solution)/shard_map/psum | solution.py:12
  92.4 63.2 %fusion = f32[32,2048]{1,0:T(8,128)} fusion(f32[2048,8192]{1,0:T(8,128)} %param.2, f32[32,2048]{1,0:T(8,128)} %get-tuple-element.25, f32[32,2048]{1,0:T(8,128)} %get-tuple-element.26, f32[32,2048]{1,0:T(8,128)} %get-tuple-element.27, f32[32,2048]{1,0:T(8,128)} %get-tuple-element.28), kind=kOutput, calls=%fused_computation | convolution fusion | flops 6443237376 | bytes 68419584 | tf_op jit(solution)/shard_map/dot_general | solution.py:20
  155.6 0.0 all-reduce.19.cloned.1.call-update
  155.6 0.0 all-reduce.39.cloned.1.call-start
  155.7 22.8 %all-reduce.19.cloned.1.call-done = f32[32,2048]{1,0:T(8,128)} async-done(((f32[32,2048]{1,0:T(8,128)}), f32[32,2048]{1,0:T(8,128)}) %all-reduce.19.cloned.1.call-update) | async-done | bytes 262160 | tf_op jit(solution)/shard_map/psum | solution.py:27
  178.5 1.9 broadcast_select_fusion.3
  180.4 0.0 all-reduce.39.cloned.1.call-update
  180.4 0.3 all-reduce.21.cloned.1.call-start
  180.8 80.1 %all-reduce.39.cloned.1.call-done = (f32[32,2048]{1,0:T(8,128)}, f32[32,2048]{1,0:T(8,128)}, f32[32,2048]{1,0:T(8,128)}, f32[32,2048]{1,0:T(8,128)}) async-done(((f32[32,2048]{1,0:T(8,128)}, f32[32,2048]{1,0:T(8,128)}, f32[32,2048]{1,0:T(8,128)}, f32[32,2048]{1,0:T(8,128)}), (f32[32,2048]{1,0:T(8,128)}, f32[32,2048]{1,0:T(8,128)}, f32[32,2048]{1,0:T(8,128)}, ...) | async-done | bytes 1048592 | tf_op jit(solution)/shard_map/psum | solution.py:12
  260.8 63.2 %fusion.8 = f32[32,2048]{1,0:T(8,128)} fusion(f32[2048,8192]{1,0:T(8,128)} %param.2, f32[32,2048]{1,0:T(8,128)} %get-tuple-element.21, f32[32,2048]{1,0:T(8,128)} %get-tuple-element.22, f32[32,2048]{1,0:T(8,128)} %get-tuple-element.23, f32[32,2048]{1,0:T(8,128)} %get-tuple-element.24), kind=kOutput, calls=%fused_computation.8 | convolution fusion | flops 6443237376 | bytes 68419584 | tf_op jit(solution)/shard_map/dot_general | solution.py:20
  324.1 0.0 all-reduce.21.cloned.1.call-update
  324.1 0.0 all-reduce.37.cloned.1.call-start
  324.1 22.8 %all-reduce.21.cloned.1.call-done = f32[32,2048]{1,0:T(8,128)} async-done(((f32[32,2048]{1,0:T(8,128)}), f32[32,2048]{1,0:T(8,128)}) %all-reduce.21.cloned.1.call-update) | async-done | bytes 262160 | tf_op jit(solution)/shard_map/psum | solution.py:27
  347.0 1.9 multiply_select_fusion.15
  348.9 0.0 all-reduce.37.cloned.1.call-update
  348.9 0.0 all-reduce.23.cloned.1.call-start
  349.0 80.1 %all-reduce.37.cloned.1.call-done = (f32[32,2048]{1,0:T(8,128)}, f32[32,2048]{1,0:T(8,128)}, f32[32,2048]{1,0:T(8,128)}, f32[32,2048]{1,0:T(8,128)}) async-done(((f32[32,2048]{1,0:T(8,128)}, f32[32,2048]{1,0:T(8,128)}, f32[32,2048]{1,0:T(8,128)}, f32[32,2048]{1,0:T(8,128)}), (f32[32,2048]{1,0:T(8,128)}, f32[32,2048]{1,0:T(8,128)}, f32[32,2048]{1,0:T(8,128)}, ...) | async-done | bytes 1048592 | tf_op jit(solution)/shard_map/psum | solution.py:12
  429.1 63.2 %fusion.16 = f32[32,2048]{1,0:T(8,128)} fusion(f32[2048,8192]{1,0:T(8,128)} %param.2, f32[32,2048]{1,0:T(8,128)} %get-tuple-element.17, f32[32,2048]{1,0:T(8,128)} %get-tuple-element.18, f32[32,2048]{1,0:T(8,128)} %get-tuple-element.19, f32[32,2048]{1,0:T(8,128)} %get-tuple-element.20), kind=kOutput, calls=%fused_computation.16 | convolution fusion | flops 6443237376 | bytes 68419584 | tf_op jit(solution)/shard_map/dot_general | solution.py:20
  492.3 0.0 all-reduce.23.cloned.1.call-update
  492.3 0.6 all-reduce.35.cloned.1.call-start
  492.9 22.3 %all-reduce.23.cloned.1.call-done = f32[32,2048]{1,0:T(8,128)} async-done(((f32[32,2048]{1,0:T(8,128)}), f32[32,2048]{1,0:T(8,128)}) %all-reduce.23.cloned.1.call-update) | async-done | bytes 262160 | tf_op jit(solution)/shard_map/psum | solution.py:27
  515.2 2.0 multiply_select_fusion.11
  517.1 0.0 all-reduce.35.cloned.1.call-update
  517.2 0.0 all-reduce.25.cloned.1.call-start
  517.2 80.3 %all-reduce.35.cloned.1.call-done = (f32[32,2048]{1,0:T(8,128)}, f32[32,2048]{1,0:T(8,128)}, f32[32,2048]{1,0:T(8,128)}, f32[32,2048]{1,0:T(8,128)}) async-done(((f32[32,2048]{1,0:T(8,128)}, f32[32,2048]{1,0:T(8,128)}, f32[32,2048]{1,0:T(8,128)}, f32[32,2048]{1,0:T(8,128)}), (f32[32,2048]{1,0:T(8,128)}, f32[32,2048]{1,0:T(8,128)}, f32[32,2048]{1,0:T(8,128)}, ...) | async-done | bytes 1048592 | tf_op jit(solution)/shard_map/psum | solution.py:12
  597.5 63.2 %fusion.24 = f32[32,2048]{1,0:T(8,128)} fusion(f32[2048,8192]{1,0:T(8,128)} %param.2, f32[32,2048]{1,0:T(8,128)} %get-tuple-element.13, f32[32,2048]{1,0:T(8,128)} %get-tuple-element.14, f32[32,2048]{1,0:T(8,128)} %get-tuple-element.15, f32[32,2048]{1,0:T(8,128)} %get-tuple-element.16), kind=kOutput, calls=%fused_computation.24 | convolution fusion | flops 6443237376 | bytes 68419584 | tf_op jit(solution)/shard_map/dot_general | solution.py:20
  660.7 0.0 all-reduce.25.cloned.1.call-update
  660.8 0.0 all-reduce.33.cloned.1.call-start
  660.8 22.8 %all-reduce.25.cloned.1.call-done = f32[32,2048]{1,0:T(8,128)} async-done(((f32[32,2048]{1,0:T(8,128)}), f32[32,2048]{1,0:T(8,128)}) %all-reduce.25.cloned.1.call-update) | async-done | bytes 262160 | tf_op jit(solution)/shard_map/psum | solution.py:27
  683.6 2.0 multiply_select_fusion.7
  685.6 0.0 all-reduce.33.cloned.1.call-update
  685.6 0.2 all-reduce.27.cloned.1.call-start
  685.8 80.2 %all-reduce.33.cloned.1.call-done = (f32[32,2048]{1,0:T(8,128)}, f32[32,2048]{1,0:T(8,128)}, f32[32,2048]{1,0:T(8,128)}, f32[32,2048]{1,0:T(8,128)}) async-done(((f32[32,2048]{1,0:T(8,128)}, f32[32,2048]{1,0:T(8,128)}, f32[32,2048]{1,0:T(8,128)}, f32[32,2048]{1,0:T(8,128)}), (f32[32,2048]{1,0:T(8,128)}, f32[32,2048]{1,0:T(8,128)}, f32[32,2048]{1,0:T(8,128)}, ...) | async-done | bytes 1048592 | tf_op jit(solution)/shard_map/psum | solution.py:12
  766.0 63.2 %fusion.32 = f32[32,2048]{1,0:T(8,128)} fusion(f32[2048,8192]{1,0:T(8,128)} %param.2, f32[32,2048]{1,0:T(8,128)} %get-tuple-element.9, f32[32,2048]{1,0:T(8,128)} %get-tuple-element.10, f32[32,2048]{1,0:T(8,128)} %get-tuple-element.11, f32[32,2048]{1,0:T(8,128)} %get-tuple-element.12), kind=kOutput, calls=%fused_computation.32 | convolution fusion | flops 6443237376 | bytes 68419584 | tf_op jit(solution)/shard_map/dot_general | solution.py:20
  829.2 0.0 copy-start
  829.2 0.0 copy-start.1
  829.2 0.0 copy-start.2
  829.2 0.0 copy-start.3
  829.2 0.0 copy-start.4
  829.3 0.0 all-reduce.27.cloned.1.call-update
  829.3 0.0 all-reduce.31.cloned.1.call-start
  829.3 22.8 %all-reduce.27.cloned.1.call-done = f32[32,2048]{1,0:T(8,128)} async-done(((f32[32,2048]{1,0:T(8,128)}), f32[32,2048]{1,0:T(8,128)}) %all-reduce.27.cloned.1.call-update) | async-done | bytes 262160 | tf_op jit(solution)/shard_map/psum | solution.py:27
  852.2 0.0 copy-start.5
  852.2 2.0 multiply_select_fusion.3
  854.2 0.0 all-reduce.31.cloned.1.call-update
  854.2 0.3 all-reduce.29.cloned.1.call-start
  854.5 80.1 %all-reduce.31.cloned.1.call-done = (f32[32,2048]{1,0:T(8,128)}, f32[32,2048]{1,0:T(8,128)}, f32[32,2048]{1,0:T(8,128)}, f32[32,2048]{1,0:T(8,128)}) async-done(((f32[32,2048]{1,0:T(8,128)}, f32[32,2048]{1,0:T(8,128)}, f32[32,2048]{1,0:T(8,128)}, f32[32,2048]{1,0:T(8,128)}), (f32[32,2048]{1,0:T(8,128)}, f32[32,2048]{1,0:T(8,128)}, f32[32,2048]{1,0:T(8,128)}, ...) | async-done | bytes 1048592 | tf_op jit(solution)/shard_map/psum | solution.py:12
  934.5 63.2 %fusion.40 = f32[32,2048]{1,0:T(8,128)} fusion(f32[2048,8192]{1,0:T(8,128)} %param.2, f32[32,2048]{1,0:T(8,128)} %get-tuple-element.5, f32[32,2048]{1,0:T(8,128)} %get-tuple-element.6, f32[32,2048]{1,0:T(8,128)} %get-tuple-element.7, f32[32,2048]{1,0:T(8,128)} %get-tuple-element.8), kind=kOutput, calls=%fused_computation.40 | convolution fusion | flops 6443237376 | bytes 68419584 | tf_op jit(solution)/shard_map/dot_general | solution.py:20
  997.8 0.0 all-reduce.29.cloned.1.call-update
  997.8 22.9 %all-reduce.29.cloned.1.call-done = f32[32,2048]{1,0:T(8,128)} async-done(((f32[32,2048]{1,0:T(8,128)}), f32[32,2048]{1,0:T(8,128)}) %all-reduce.29.cloned.1.call-update) | async-done | bytes 262160 | tf_op jit(solution)/shard_map/psum | solution.py:27
  1020.6 0.0 copy-done
  1020.6 0.0 copy-done.1
  1020.7 0.0 copy-done.2
  1020.7 0.0 copy-done.3
  1020.7 0.0 copy-done.4
  1020.7 0.0 copy-done.5
  1020.7 1.8 multiply_add_fusion
Async XLA Ops:
  6.5 85.8 %all-reduce.41.cloned.1.call-start = ((), (), s32[]{:S(2)}) async-start(), calls=%async_computation.11 | async-start | bytes 2097152 | tf_op jit(solution)/shard_map/psum | solution.py:12
  8.5 170.0 %all-reduce.19.cloned.1.call-start = ((), (), s32[]{:S(2)}) async-start(), calls=%async_computation | async-start | bytes 524288 | tf_op jit(solution)/shard_map/psum | solution.py:27
  155.6 105.2 %all-reduce.39.cloned.1.call-start = ((), (), s32[]{:S(2)}) async-start(), calls=%async_computation.10 | async-start | bytes 2097152 | tf_op jit(solution)/shard_map/psum | solution.py:12
  180.4 166.5 %all-reduce.21.cloned.1.call-start = ((), (), s32[]{:S(2)}) async-start(), calls=%async_computation.1 | async-start | bytes 524288 | tf_op jit(solution)/shard_map/psum | solution.py:27
  324.1 105.0 %all-reduce.37.cloned.1.call-start = ((), (), s32[]{:S(2)}) async-start(), calls=%async_computation.9 | async-start | bytes 2097152 | tf_op jit(solution)/shard_map/psum | solution.py:12
  348.9 166.3 %all-reduce.23.cloned.1.call-start = ((), (), s32[]{:S(2)}) async-start(), calls=%async_computation.2 | async-start | bytes 524288 | tf_op jit(solution)/shard_map/psum | solution.py:27
  492.3 105.2 %all-reduce.35.cloned.1.call-start = ((), (), s32[]{:S(2)}) async-start(), calls=%async_computation.8 | async-start | bytes 2097152 | tf_op jit(solution)/shard_map/psum | solution.py:12
  517.2 166.5 %all-reduce.25.cloned.1.call-start = ((), (), s32[]{:S(2)}) async-start(), calls=%async_computation.3 | async-start | bytes 524288 | tf_op jit(solution)/shard_map/psum | solution.py:27
  660.8 105.2 %all-reduce.33.cloned.1.call-start = ((), (), s32[]{:S(2)}) async-start(), calls=%async_computation.7 | async-start | bytes 2097152 | tf_op jit(solution)/shard_map/psum | solution.py:12
  685.6 166.5 %all-reduce.27.cloned.1.call-start = ((), (), s32[]{:S(2)}) async-start(), calls=%async_computation.4 | async-start | bytes 524288 | tf_op jit(solution)/shard_map/psum | solution.py:27
  829.2 191.4 %copy-start = (f32[32,2048]{1,0:T(8,128)S(1)}, f32[32,2048]{1,0:T(8,128)}, u32[]{:S(2)}) copy-start(f32[32,2048]{1,0:T(8,128)} %param.3) | copy-start | bytes 786436
  829.2 191.4 %copy-start.1 = (f32[32,2048]{1,0:T(8,128)S(1)}, f32[32,2048]{1,0:T(8,128)}, u32[]{:S(2)}) copy-start(f32[32,2048]{1,0:T(8,128)} %all-reduce.19.cloned.1.call-done) | copy-start | bytes 786436
  829.2 191.4 %copy-start.2 = (f32[32,2048]{1,0:T(8,128)S(1)}, f32[32,2048]{1,0:T(8,128)}, u32[]{:S(2)}) copy-start(f32[32,2048]{1,0:T(8,128)} %all-reduce.21.cloned.1.call-done) | copy-start | bytes 786436
  829.2 191.4 %copy-start.3 = (f32[32,2048]{1,0:T(8,128)S(1)}, f32[32,2048]{1,0:T(8,128)}, u32[]{:S(2)}) copy-start(f32[32,2048]{1,0:T(8,128)} %all-reduce.23.cloned.1.call-done) | copy-start | bytes 786436
  829.2 191.4 %copy-start.4 = (f32[32,2048]{1,0:T(8,128)S(1)}, f32[32,2048]{1,0:T(8,128)}, u32[]{:S(2)}) copy-start(f32[32,2048]{1,0:T(8,128)} %all-reduce.25.cloned.1.call-done) | copy-start | bytes 786436
  829.3 105.2 %all-reduce.31.cloned.1.call-start = ((), (), s32[]{:S(2)}) async-start(), calls=%async_computation.6 | async-start | bytes 2097152 | tf_op jit(solution)/shard_map/psum | solution.py:12
  852.2 168.5 %copy-start.5 = (f32[32,2048]{1,0:T(8,128)S(1)}, f32[32,2048]{1,0:T(8,128)}, u32[]{:S(2)}) copy-start(f32[32,2048]{1,0:T(8,128)} %all-reduce.27.cloned.1.call-done) | copy-start | bytes 786436
  854.2 166.4 %all-reduce.29.cloned.1.call-start = ((), (), s32[]{:S(2)}) async-start(), calls=%async_computation.5 | async-start | bytes 524288 | tf_op jit(solution)/shard_map/psum | solution.py:27
Sparse Core Ops, SparseCore 0:
  11.2 81.1 all-reduce.40
  155.7 22.7 all-reduce.18
  182.3 78.4 all-reduce.38
  324.2 22.7 all-reduce.20
  350.7 78.3 all-reduce.36
  492.4 22.7 all-reduce.22
  519.0 78.4 all-reduce.34
  660.9 22.7 all-reduce.24
  687.5 78.4 all-reduce.32
  829.4 22.7 all-reduce.26
  856.0 78.4 all-reduce.30
  997.9 22.7 all-reduce.28
where the time goes:
time: 1030 us
  waiting for transfers between devices  621 us (60%)
  matrix products  379 us (37%)
  between operations  13.8 us (1%)
  other arithmetic  13.5 us (1%)
    psum x6, waiting for transfers between devices, broadcast(): return lax.psum(block, axis)  484 us
    dot_general x6, matrix products, apply_matrix(): lax.dot_general(operand, matrix, (((1,), (1,)), ((), ())), precision=lax....  379 us
    psum x6, waiting for transfers between devices, apply_matrix(): return lax.psum(partial_value, 'col')  136 us
  transfers between devices with their start and end apart: 12, of which 12 were waited for; matrix products, arithmetic and copies ran while one was open for 0% of the time, Pallas kernels for 0%

commit v1 on v0

v1 whole, which is shorter than its diff:
```python
import functools

import jax
import jax.numpy as jnp
from jax import lax
from jax.experimental import pallas as pl
from jax.experimental.pallas import tpu as pltpu
from jax.sharding import PartitionSpec as P


TERMS = 6
STEPS = 1
AXES = ("row", "col", "rep")
CHUNKS = 2
RING = 12


def split_kernel(fan, parts, matrix, *refs):
    outs, ring, sems = refs[: 2 * fan], refs[2 * fan], refs[2 * fan + 1]
    slots, step, depth = ring.shape
    rep, seat = lax.axis_index("rep"), lax.axis_index("row") % fan
    blocks = matrix.shape[0] // step
    each = blocks // parts
    total = fan * blocks
    tile = min(256, depth)
    shape = (tile, tile)
    diagonal = lax.broadcasted_iota(jnp.int32, shape, 0) == lax.broadcasted_iota(jnp.int32, shape, 1)
    identity = jnp.where(diagonal, 1.0, 0.0).astype(jnp.bfloat16)

    def copy(t):
        block = t % blocks
        row = pl.multiple_of(((rep ^ (block // each)) * each + block % each) * step, step)
        column = pl.multiple_of(((seat ^ (t // blocks)) * parts + rep) * depth, depth)
        slot = t % slots
        return pltpu.make_async_copy(
            matrix.at[pl.ds(row, step), pl.ds(column, depth)], ring.at[slot], sems.at[slot]
        )

    for t in range(min(slots, total)):
        copy(t).start()
    for q in range(fan):

        @pl.loop(0, blocks)
        def _(block, q=q):
            t = q * blocks + block
            copy(t).wait()
            value = ring[t % slots]
            top = value.astype(jnp.bfloat16)
            rest = (value - top.astype(jnp.float32)).astype(jnp.bfloat16)
            column = pl.multiple_of(block * step, step)
            for source, out in ((top, outs[2 * q]), (rest, outs[2 * q + 1])):
                for at in range(0, depth, tile):
                    turned = lax.dot_general(
                        identity,
                        source[:, at : at + tile],
                        (((1,), (1,)), ((), ())),
                        preferred_element_type=jnp.float32,
                    )
                    out[at : at + tile, pl.ds(column, step)] = turned.astype(jnp.bfloat16)

            @pl.when(t + slots < total)
            def _():
                copy(t + slots).start()


def split_matrix(matrix, fan, parts, depth):
    rows = matrix.shape[0]
    step = min(256, rows // parts)
    outs = pl.pallas_call(
        functools.partial(split_kernel, fan, parts),
        out_shape=(pltpu.VMEM((depth, rows), jnp.bfloat16),) * (2 * fan),
        in_specs=[pl.BlockSpec(memory_space=pl.ANY)],
        out_specs=(pl.BlockSpec(memory_space=pltpu.VMEM),) * (2 * fan),
        scratch_shapes=[
            pltpu.VMEM((RING, step, depth), jnp.float32),
            pltpu.SemaphoreType.DMA((RING,)),
        ],
        compiler_params=pltpu.CompilerParams(vmem_limit_bytes=20 << 20),
        cost_estimate=pl.CostEstimate(
            flops=8 * rows * depth * fan, bytes_accessed=4 * rows * depth * fan, transcendentals=0
        ),
        name="split",
    )(matrix)
    return list(zip(outs[::2], outs[1::2]))


def product_kernel(ranges, chunks, first, *refs):
    refs = list(refs)
    before = None if first else [refs.pop(0) for _ in ranges]
    value = jnp.concatenate([refs.pop(0)[...] for _ in range(chunks)], axis=1)
    upper, lower = refs.pop(0), refs.pop(0)
    count = value.shape[0]
    high = value.astype(jnp.bfloat16)
    low = (value - high.astype(jnp.float32)).astype(jnp.bfloat16)
    both = jnp.concatenate([high, low], axis=0)
    for place, (start, width) in enumerate(ranges):
        here = slice(start, start + width)
        main = jnp.dot(both, upper[:, here], preferred_element_type=jnp.float32)
        rest = jnp.dot(high, lower[:, here], preferred_element_type=jnp.float32)
        total = main[:count] + (main[count:] + rest)
        refs[place][...] = total if first else before[place][...] + total


def product(before, pieces, weights, ranges):
    count, depth = pieces[0].shape[0], weights[0].shape[0]
    width = sum(w for _, w in ranges)
    operands = list(before or []) + list(pieces) + list(weights)
    vmem = pl.BlockSpec(memory_space=pltpu.VMEM)
    return pl.pallas_call(
        functools.partial(product_kernel, ranges, len(pieces), before is None),
        out_shape=tuple(jax.ShapeDtypeStruct((count, w), jnp.float32) for _, w in ranges),
        in_specs=[vmem] * len(operands),
        out_specs=(vmem,) * len(ranges),
        input_output_aliases={} if before is None else {i: i for i in range(len(ranges))},
        compiler_params=pltpu.CompilerParams(vmem_limit_bytes=16 << 20),
        cost_estimate=pl.CostEstimate(
            flops=6 * count * depth * width,
            bytes_accessed=4 * depth * width,
            transcendentals=0,
        ),
        name="product",
    )(*operands)


def whole_call(kernel, outs, *operands):
    vmem = pl.BlockSpec(memory_space=pltpu.VMEM)
    return pl.pallas_call(
        kernel,
        out_shape=tuple(jax.ShapeDtypeStruct(shape, jnp.float32) for shape in outs),
        in_specs=[vmem] * len(operands),
        out_specs=(vmem,) * len(outs),
        compiler_params=pltpu.CompilerParams(vmem_limit_bytes=16 << 20),
    )(*operands)


def deal_kernel(vectors, *outs):
    rep = lax.axis_index("rep")
    width = outs[0].shape[1]
    for q, out in enumerate(outs):
        at = pl.multiple_of((rep ^ q) * width, width)
        out[...] = vectors[:, pl.ds(at, width)]


def sort_kernel(parts, *refs):
    rep = lax.axis_index("rep")
    values = [ref[...] for ref in refs[:parts]]
    size = values[0].shape[0]
    width = refs[parts].shape[1]
    for p in range(parts):
        value = values[0]
        for q in range(1, parts):
            value = jnp.where((rep ^ q) == p, values[q], value)
        for h, out in enumerate(refs[parts:]):
            out[p * size : (p + 1) * size, :] = value[:, h * width : (h + 1) * width]


def close_kernel(fan, parts, chunks, scale, *refs):
    count = parts * chunks
    sums, running, outs = refs[:count], refs[count : count + chunks], refs[count + chunks :]
    rep = lax.axis_index("rep")
    home = (lax.axis_index("row") // fan) == lax.axis_index("col")
    size, width = outs[0].shape[0], running[0].shape[1]
    for p in range(parts):
        for h in range(chunks):
            for v in range(parts):
                rows = slice(v * size, (v + 1) * size)
                value = sums[p * chunks + h][rows, :] * scale
                if p == 0:
                    value = value + jnp.where(home, running[h][rows, :], 0.0)
                at = pl.multiple_of((rep ^ p) * (width * chunks) + h * width, width)
                for q in range(parts):

                    @pl.when((rep ^ q) == v)
                    def _(value=value, out=outs[q], at=at):
                        out[:, pl.ds(at, width)] = value


def local(matrix, vectors):
    across, cols, parts = (lax.axis_size(axis) for axis in AXES)
    fan = across // cols
    count, rows = vectors.shape[0] * parts, vectors.shape[1]
    depth, size = rows // parts, vectors.shape[0]
    width = depth // CHUNKS

    def move(value, target):
        pairs = []
        for r in range(across):
            for c in range(cols):
                for k in range(parts):
                    h, s, d, e = target(r // fan, r % fan, c, k)
                    pairs.append(
                        ((r * cols + c) * parts + k, ((h * fan + s) * cols + d) * parts + e)
                    )
        return lax.ppermute(value, AXES, pairs)

    def swap_rep(value, q):
        return move(value, lambda h, s, c, k: (h, s, c, k ^ q))

    def swap_col(value, q):
        return move(value, lambda h, s, c, k: (h, s, c ^ q, k))

    def to_plane(value, q):
        return move(value, lambda h, s, c, k: ((c - q) % cols, s, h, k))

    def swap_seat(value, q):
        return move(value, lambda h, s, c, k: (h, s ^ q, c, k))

    slots = list(whole_call(deal_kernel, [(size, depth)] * parts, vectors))
    slots = [slots[0]] + [swap_rep(slots[q], q) for q in range(1, parts)]
    pieces = whole_call(functools.partial(sort_kernel, parts), [(count, width)] * CHUNKS, *slots)

    ranges = tuple((p * depth + h * width, width) for p in range(parts) for h in range(CHUNKS))
    running = None
    for degree in range(1, TERMS + 1):
        if degree == 1:
            own = [to_plane(piece, cols - 1) for piece in pieces]
            running = own
            weights = split_matrix(matrix, fan, parts, depth)
        else:
            own = []
            for piece in pieces:
                moved = [to_plane(piece, q) for q in reversed(range(cols))]
                own.append(sum(moved[1:], moved[0]) * scale)
            running = [a + b for a, b in zip(running, own)]
        groups = [own]
        for q in range(1, fan):
            groups.append([swap_seat(piece, q) for piece in own])
        sums = None
        for at in range(fan - 1):
            sums = product(sums, groups[at], weights[at], ranges)
        last = [None] * len(ranges)
        for h in range(CHUNKS):
            places = range(h, len(ranges), CHUNKS)
            done = product(
                None if sums is None else [sums[i] for i in places],
                groups[-1],
                weights[-1],
                tuple(ranges[i] for i in places),
            )
            for i, value in zip(places, done):
                last[i] = value
        sums = last
        scale = 1.0 / float(degree * STEPS)
        if degree < TERMS:
            pieces = []
            for h in range(CHUNKS):
                total = sums[h]
                for q in range(1, parts):
                    total = total + swap_rep(sums[q * CHUNKS + h], q)
                pieces.append(total)
    outs = whole_call(
        functools.partial(close_kernel, fan, parts, CHUNKS, scale),
        [(size, rows)] * parts,
        *sums,
        *running,
    )
    result = outs[0]
    for q in range(1, parts):
        result = result + swap_rep(outs[q], q)
    q = 1
    while q < cols:
        result = result + swap_col(result, q)
        q *= 2
    return result


def solution(mesh):
    placed = (P("row", "col"), P("rep", "row"))
    return jax.shard_map(
        local, mesh=mesh, in_specs=placed, out_specs=P("rep", "row"), check_vma=False
    )
```

time: 1030 us -> 237 us (0.23)
  waiting for transfers between devices: 621 us -> 49 us
  matrix products: 379 us -> 0 us
  starting transfers between devices: 1.66 us -> 130 us
  Pallas kernels: 0 us -> 54.1 us
  between operations: 13.8 us -> 0.69 us
  other arithmetic: 13.5 us -> 1.28 us
    psum x12 -> x0, waiting for transfers between devices: 621 us -> none  [the longest x6 484 us: broadcast(): return lax.psum(block, axis)]
    dot_general x6 -> x0, matrix products: 379 us -> none  [apply_matrix(): lax.dot_general(operand, matrix, (((1,), (1,)), ((), ())), precision=lax....]
    ppermute x0 -> x71, starting transfers between devices: none -> 130 us  [move(): return lax.ppermute(value, AXES, pairs)]
    pallas_call x0 -> x34, Pallas kernels: none -> 54.1 us  [the longest x30 37.1 us: product(): pl.pallas_call(functools.partial(product_kernel, ranges, len(pieces), bef...]
    ppermute x0 -> x71, waiting for transfers between devices: none -> 49 us  [move(): return lax.ppermute(value, AXES, pairs)]
    select_n x6 -> x0, other arithmetic: 11.8 us -> none  [broadcast(): jnp.where(lax.axis_index(axis) == holder, block, jnp.zeros_like(block))]
  transfers between devices with their start and end apart: 12 -> 71, of which waited for: 12 -> 32; matrix products, arithmetic and copies ran while one was open for 0% -> 0% of each run, Pallas kernels for 0% -> 20%
where the time goes in v1:
time: 237 us; the launch traced here: 236 us
  starting transfers between devices  130 us (55%)
  Pallas kernels  54.1 us (23%)
  waiting for transfers between devices  49 us (21%)
    ppermute x71, starting transfers between devices, move(): return lax.ppermute(value, AXES, pairs)  130 us
    ppermute x71, waiting for transfers between devices, move(): return lax.ppermute(value, AXES, pairs)  49 us
    pallas_call x30, Pallas kernels, product(): pl.pallas_call(functools.partial(product_kernel, ranges, len(pieces), bef...  37.1 us
    pallas_call x1, Pallas kernels, split_matrix(): pl.pallas_call(functools.partial(split_kernel, fan, parts), out_shape=(pl...  16.9 us
  transfers between devices with their start and end apart: 71, of which 32 were waited for; matrix products, arithmetic and copies ran while one was open for 0% of the time, Pallas kernels for 20%

profile of v1, /device:TPU:0, one launch (start us, length us, event | category | flops | bytes accessed | tf_op | source)
XLA Modules:
  0.0 235.9 jit_solution(722893381988189058)
XLA Ops:
  2.5 4.0 %collective-permute-start.1 = (f32[64,512]{1,0:T(8,128)S(1)}, f32[64,512]{1,0:T(8,128)S(1)}, u32[]{:S(2)}, u32[]{:S(2)}) collective-permute-start(f32[64,512]{1,0:T(8,128)S(1)} %get-tuple-element.117), channel_id=1, source_target_pairs={{0,16},{1,17},{2,0},{3,1},{4,20},{5,21},{6,4},{7,5},{8,24},{9,25},... | collective-permute-start | bytes 393224 | tf_op jit(solution)/shard_map/ppermute | solution.py:194
  6.5 1.5 collective-permute-start.2
  8.1 2.4 %collective-permute-done.1.refs_0_ = f32[64,512]{1,0:T(8,128)S(1)} collective-permute-done((f32[64,512]{1,0:T(8,128)S(1)}, f32[64,512]{1,0:T(8,128)S(1)}, u32[]{:S(2)}, u32[]{:S(2)}) %collective-permute-start.1) | collective-permute-done | bytes 131104 | tf_op jit(solution)/shard_map/ppermute | solution.py:194
  10.5 1.5 collective-permute-start.3
  12.5 1.5 collective-permute-start.4
  13.9 16.9 %split.1 = (bf16[1024,2048]{1,0:T(8,128)(2,1)S(1)}, bf16[1024,2048]{1,0:T(8,128)(2,1)S(1)}, bf16[1024,2048]{1,0:T(8,128)(2,1)S(1)}, bf16[1024,2048]{1,0:T(8,128)...) custom-call(f32[2048,8192]{1,0:T(8,128)} %matrix.1), custom_call_target="tpu_custom_call" | custom-call | flops 67108864 | bytes 33554432 | tf_op jit(solution)/shard_map/split/pallas_call | solution.py:69
  30.9 7.1 %collective-permute-start.5 = (f32[64,512]{1,0:T(8,128)S(1)}, f32[64,512]{1,0:T(8,128)S(1)}, u32[]{:S(2)}, u32[]{:S(2)}) collective-permute-start(f32[64,512]{1,0:T(8,128)S(1)} %collective-permute-done.1.refs_0_), channel_id=1, source_target_pairs={{0,8},{1,9},{2,10},{3,11},{4,12},{5,13},{6,14},{7,15},{8,0},{9,1},... | collective-permute-start | bytes 393224 | tf_op jit(solution)/shard_map/ppermute | solution.py:194
  38.1 1.9 collective-permute-start.7
  40.0 1.5 product.30
  42.6 1.5 product.31
  45.1 1.5 product.32
  47.9 1.9 collective-permute-done.8.refs_3_
  52.1 3.4 %collective-permute-start.13 = (f32[64,512]{1,0:T(8,128)S(1)}, f32[64,512]{1,0:T(8,128)S(1)}, u32[]{:S(2)}, u32[]{:S(2)}) collective-permute-start(f32[64,512]{1,0:T(8,128)S(1)} %add.98), channel_id=1, source_target_pairs={{0,16},{1,17},{2,0},{3,1},{4,20},{5,21},{6,4},{7,5},{8,24},{9,25},... | collective-permute-start | bytes 393224 | tf_op jit(solution)/shard_map/ppermute | solution.py:194
  56.2 2.3 collective-permute-start.10
  59.4 1.6 collective-permute-start.16
  61.0 1.5 collective-permute-done.10
  62.5 1.6 collective-permute-start.15
  64.1 5.9 %collective-permute-start.18 = (f32[64,512]{1,0:T(8,128)S(1)}, f32[64,512]{1,0:T(8,128)S(1)}, u32[]{:S(2)}, u32[]{:S(2)}) collective-permute-start(f32[64,512]{1,0:T(8,128)S(1)} %add.99.refs_1_), channel_id=1, source_target_pairs={{0,8},{1,9},{2,10},{3,11},{4,12},{5,13},{6,14},{7,15},{8,0},{9,1},... | collective-permute-start | bytes 393224 | tf_op jit(solution)/shard_map/ppermute | solution.py:194
  70.0 2.0 collective-permute-start.20
  72.0 1.5 product.35
  74.5 1.5 product.36
  77.2 1.5 product.37
  79.9 2.4 %collective-permute-done.19.refs_2_ = f32[64,512]{1,0:T(8,128)S(1)} collective-permute-done((f32[64,512]{1,0:T(8,128)S(1)}, f32[64,512]{1,0:T(8,128)S(1)}, u32[]{:S(2)}, u32[]{:S(2)}) %collective-permute-start.19) | collective-permute-done | bytes 131104 | tf_op jit(solution)/shard_map/ppermute | solution.py:194
  84.6 5.8 %collective-permute-start.25 = (f32[64,512]{1,0:T(8,128)S(1)}, f32[64,512]{1,0:T(8,128)S(1)}, u32[]{:S(2)}, u32[]{:S(2)}) collective-permute-start(f32[64,512]{1,0:T(8,128)S(1)} %add.102), channel_id=1, source_target_pairs={{0,16},{1,17},{2,0},{3,1},{4,20},{5,21},{6,4},{7,5},{8,24},{9,25},... | collective-permute-start | bytes 393224 | tf_op jit(solution)/shard_map/ppermute | solution.py:194
  91.1 1.6 collective-permute-start.22
  94.3 1.6 collective-permute-start.28
  95.9 1.5 collective-permute-done.22
  97.4 1.6 collective-permute-start.27
  99.0 5.9 %collective-permute-start.30 = (f32[64,512]{1,0:T(8,128)S(1)}, f32[64,512]{1,0:T(8,128)S(1)}, u32[]{:S(2)}, u32[]{:S(2)}) collective-permute-start(f32[64,512]{1,0:T(8,128)S(1)} %add_multiply_fusion.6.refs_1_), channel_id=1, source_target_pairs={{0,8},{1,9},{2,10},{3,11},{4,12},{5,13},{6,14},{7,15},{8,0},{9,1},... | collective-permute-start | bytes 393224 | tf_op jit(solution)/shard_map/ppermute | solution.py:194
  104.9 2.0 collective-permute-start.32
  106.9 1.5 product.40
  109.4 1.5 product.41
  112.1 1.5 product.42
  114.8 1.9 collective-permute-done.31.refs_2_
  119.0 6.3 %collective-permute-start.37 = (f32[64,512]{1,0:T(8,128)S(1)}, f32[64,512]{1,0:T(8,128)S(1)}, u32[]{:S(2)}, u32[]{:S(2)}) collective-permute-start(f32[64,512]{1,0:T(8,128)S(1)} %add.106), channel_id=1, source_target_pairs={{0,16},{1,17},{2,0},{3,1},{4,20},{5,21},{6,4},{7,5},{8,24},{9,25},... | collective-permute-start | bytes 393224 | tf_op jit(solution)/shard_map/ppermute | solution.py:194
  129.2 1.6 collective-permute-start.40
  130.8 1.5 collective-permute-done.34
  132.3 1.6 collective-permute-start.39
  133.9 5.9 %collective-permute-start.42 = (f32[64,512]{1,0:T(8,128)S(1)}, f32[64,512]{1,0:T(8,128)S(1)}, u32[]{:S(2)}, u32[]{:S(2)}) collective-permute-start(f32[64,512]{1,0:T(8,128)S(1)} %add_multiply_fusion.4.refs_1_), channel_id=1, source_target_pairs={{0,8},{1,9},{2,10},{3,11},{4,12},{5,13},{6,14},{7,15},{8,0},{9,1},... | collective-permute-start | bytes 393224 | tf_op jit(solution)/shard_map/ppermute | solution.py:194
  139.8 2.0 collective-permute-start.44
  144.3 1.5 product.46
  147.0 1.5 product.47
  149.7 1.9 collective-permute-done.43.refs_2_
  153.9 6.3 %collective-permute-start.49 = (f32[64,512]{1,0:T(8,128)S(1)}, f32[64,512]{1,0:T(8,128)S(1)}, u32[]{:S(2)}, u32[]{:S(2)}) collective-permute-start(f32[64,512]{1,0:T(8,128)S(1)} %add.110), channel_id=1, source_target_pairs={{0,16},{1,17},{2,0},{3,1},{4,20},{5,21},{6,4},{7,5},{8,24},{9,25},... | collective-permute-start | bytes 393224 | tf_op jit(solution)/shard_map/ppermute | solution.py:194
  164.1 1.6 collective-permute-start.52
  165.6 1.5 collective-permute-done.46
  167.2 1.6 collective-permute-start.51
  168.7 5.9 %collective-permute-start.54 = (f32[64,512]{1,0:T(8,128)S(1)}, f32[64,512]{1,0:T(8,128)S(1)}, u32[]{:S(2)}, u32[]{:S(2)}) collective-permute-start(f32[64,512]{1,0:T(8,128)S(1)} %add_multiply_fusion.2.refs_1_), channel_id=1, source_target_pairs={{0,8},{1,9},{2,10},{3,11},{4,12},{5,13},{6,14},{7,15},{8,0},{9,1},... | collective-permute-start | bytes 393224 | tf_op jit(solution)/shard_map/ppermute | solution.py:194
  174.7 2.0 collective-permute-start.56
  176.7 1.5 product.50
  179.2 1.5 product.51
  181.8 1.5 product.52
  184.6 1.9 collective-permute-done.55.refs_2_
  188.8 6.3 %collective-permute-start.61 = (f32[64,512]{1,0:T(8,128)S(1)}, f32[64,512]{1,0:T(8,128)S(1)}, u32[]{:S(2)}, u32[]{:S(2)}) collective-permute-start(f32[64,512]{1,0:T(8,128)S(1)} %add.114), channel_id=1, source_target_pairs={{0,16},{1,17},{2,0},{3,1},{4,20},{5,21},{6,4},{7,5},{8,24},{9,25},... | collective-permute-start | bytes 393224 | tf_op jit(solution)/shard_map/ppermute | solution.py:194
  199.0 1.6 collective-permute-start.64
  202.1 1.6 collective-permute-start.63
  203.7 5.9 %collective-permute-start.66 = (f32[64,512]{1,0:T(8,128)S(1)}, f32[64,512]{1,0:T(8,128)S(1)}, u32[]{:S(2)}, u32[]{:S(2)}) collective-permute-start(f32[64,512]{1,0:T(8,128)S(1)} %get-tuple-element.226.refs_1_), channel_id=1, source_target_pairs={{0,8},{1,9},{2,10},{3,11},{4,12},{5,13},{6,14},{7,15},{8,0},{9,1},... | collective-permute-start | bytes 393224 | tf_op jit(solution)/shard_map/ppermute | solution.py:194
  209.7 1.9 collective-permute-start.68
  214.2 1.5 product.56
  216.8 1.5 product.57
  219.5 1.9 collective-permute-done.67.refs_2_
  223.3 1.5 collective-permute-done.69
  224.8 3.7 %collective-permute-start.70 = (f32[32,2048]{1,0:T(8,128)S(1)}, f32[32,2048]{1,0:T(8,128)S(1)}, u32[]{:S(2)}, u32[]{:S(2)}) collective-permute-start(f32[32,2048]{1,0:T(8,128)S(1)} %add.126), channel_id=1, source_target_pairs={{0,2},{1,3},{2,0},{3,1},{4,6},{5,7},{6,4},{7,5},{8,10},{9,11},{10,... | collective-permute-start | bytes 786440 | tf_op jit(solution)/shard_map/ppermute | solution.py:194
  228.6 6.6 %collective-permute-done.70 = f32[32,2048]{1,0:T(8,128)S(1)} collective-permute-done((f32[32,2048]{1,0:T(8,128)S(1)}, f32[32,2048]{1,0:T(8,128)S(1)}, u32[]{:S(2)}, u32[]{:S(2)}) %collective-permute-start.70) | collective-permute-done | bytes 262176 | tf_op jit(solution)/shard_map/ppermute | solution.py:194
  (136 shorter events, 57.3 us)
Async XLA Ops:
  2.5 7.9 %collective-permute-start.1 = (f32[64,512]{1,0:T(8,128)S(1)}, f32[64,512]{1,0:T(8,128)S(1)}, u32[]{:S(2)}, u32[]{:S(2)}) collective-permute-start(f32[64,512]{1,0:T(8,128)S(1)} %get-tuple-element.117), channel_id=1, source_target_pairs={{0,16},{1,17},{2,0},{3,1},{4,20},{5,21},{6,4},{7,5},{8,24},{9,25},... | collective-permute-start | bytes 393224 | tf_op jit(solution)/shard_map/ppermute | solution.py:194
  6.5 5.9 %collective-permute-start.2 = (f32[64,512]{1,0:T(8,128)S(1)}, f32[64,512]{1,0:T(8,128)S(1)}, u32[]{:S(2)}, u32[]{:S(2)}) collective-permute-start(f32[64,512]{1,0:T(8,128)S(1)} %get-tuple-element.118), channel_id=1, source_target_pairs={{0,16},{1,17},{2,0},{3,1},{4,20},{5,21},{6,4},{7,5},{8,24},{9,25},... | collective-permute-start | bytes 393224 | tf_op jit(solution)/shard_map/ppermute | solution.py:194
  10.5 31.0 %collective-permute-start.3 = (f32[64,512]{1,0:T(8,128)S(1)}, f32[64,512]{1,0:T(8,128)S(1)}, u32[]{:S(2)}, u32[]{:S(2)}) collective-permute-start(f32[64,512]{1,0:T(8,128)S(1)} %collective-permute-done.1.refs_0_), channel_id=1, source_target_pairs={{0,4},{1,5},{2,6},{3,7},{4,0},{5,1},{6,2},{7,3},{8,12},{9,13},{10,... | collective-permute-start | bytes 393224 | tf_op jit(solution)/shard_map/ppermute | solution.py:194
  12.5 30.1 %collective-permute-start.4 = (f32[64,512]{1,0:T(8,128)S(1)}, f32[64,512]{1,0:T(8,128)S(1)}, u32[]{:S(2)}, u32[]{:S(2)}) collective-permute-start(f32[64,512]{1,0:T(8,128)S(1)} %collective-permute-done.2.refs_1_), channel_id=1, source_target_pairs={{0,4},{1,5},{2,6},{3,7},{4,0},{5,1},{6,2},{7,3},{8,12},{9,13},{10,... | collective-permute-start | bytes 393224 | tf_op jit(solution)/shard_map/ppermute | solution.py:194
  30.9 13.2 %collective-permute-start.5 = (f32[64,512]{1,0:T(8,128)S(1)}, f32[64,512]{1,0:T(8,128)S(1)}, u32[]{:S(2)}, u32[]{:S(2)}) collective-permute-start(f32[64,512]{1,0:T(8,128)S(1)} %collective-permute-done.1.refs_0_), channel_id=1, source_target_pairs={{0,8},{1,9},{2,10},{3,11},{4,12},{5,13},{6,14},{7,15},{8,0},{9,1},... | collective-permute-start | bytes 393224 | tf_op jit(solution)/shard_map/ppermute | solution.py:194
  38.0 7.2 %collective-permute-start.6 = (f32[64,512]{1,0:T(8,128)S(1)}, f32[64,512]{1,0:T(8,128)S(1)}, u32[]{:S(2)}, u32[]{:S(2)}) collective-permute-start(f32[64,512]{1,0:T(8,128)S(1)} %collective-permute-done.2.refs_1_), channel_id=1, source_target_pairs={{0,8},{1,9},{2,10},{3,11},{4,12},{5,13},{6,14},{7,15},{8,0},{9,1},... | collective-permute-start | bytes 393224 | tf_op jit(solution)/shard_map/ppermute | solution.py:194
  38.1 9.9 %collective-permute-start.7 = (f32[64,512]{1,0:T(8,128)S(1)}, f32[64,512]{1,0:T(8,128)S(1)}, u32[]{:S(2)}, u32[]{:S(2)}) collective-permute-start(f32[64,512]{1,0:T(8,128)S(1)} %collective-permute-done.1.refs_0_), channel_id=1, source_target_pairs={{0,12},{1,13},{2,14},{3,15},{4,8},{5,9},{6,10},{7,11},{8,4},{9,5},... | collective-permute-start | bytes 393224 | tf_op jit(solution)/shard_map/ppermute | solution.py:194
  41.5 8.3 %collective-permute-start.8 = (f32[64,512]{1,0:T(8,128)S(1)}, f32[64,512]{1,0:T(8,128)S(1)}, u32[]{:S(2)}, u32[]{:S(2)}) collective-permute-start(f32[64,512]{1,0:T(8,128)S(1)} %collective-permute-done.2.refs_1_), channel_id=1, source_target_pairs={{0,12},{1,13},{2,14},{3,15},{4,8},{5,9},{6,10},{7,11},{8,4},{9,5},... | collective-permute-start | bytes 393224 | tf_op jit(solution)/shard_map/ppermute | solution.py:194
  51.5 4.7 %collective-permute-start.9 = (f32[64,512]{1,0:T(8,128)S(1)}, f32[64,512]{1,0:T(8,128)S(1)}, u32[]{:S(2)}, u32[]{:S(2)}) collective-permute-start(f32[64,512]{1,0:T(8,128)S(1)} %get-tuple-element.138), channel_id=1, source_target_pairs={{0,1},{1,0},{2,3},{3,2},{4,5},{5,4},{6,7},{7,6},{8,9},{9,8},{10,11... | collective-permute-start | bytes 393224 | tf_op jit(solution)/shard_map/ppermute | solution.py:194
  52.1 7.3 %collective-permute-start.13 = (f32[64,512]{1,0:T(8,128)S(1)}, f32[64,512]{1,0:T(8,128)S(1)}, u32[]{:S(2)}, u32[]{:S(2)}) collective-permute-start(f32[64,512]{1,0:T(8,128)S(1)} %add.98), channel_id=1, source_target_pairs={{0,16},{1,17},{2,0},{3,1},{4,20},{5,21},{6,4},{7,5},{8,24},{9,25},... | collective-permute-start | bytes 393224 | tf_op jit(solution)/shard_map/ppermute | solution.py:194
  55.5 3.9 %collective-permute-start.14 = (f32[64,512]{1,0:T(8,128)S(1)}, f32[64,512]{1,0:T(8,128)S(1)}, u32[]{:S(2)}, u32[]{:S(2)}) collective-permute-start(f32[64,512]{1,0:T(8,128)S(1)} %add.98), channel_id=1, source_target_pairs={{0,0},{1,1},{2,16},{3,17},{4,4},{5,5},{6,20},{7,21},{8,8},{9,9},{1... | collective-permute-start | bytes 393224 | tf_op jit(solution)/shard_map/ppermute | solution.py:194
  56.2 6.3 %collective-permute-start.10 = (f32[64,512]{1,0:T(8,128)S(1)}, f32[64,512]{1,0:T(8,128)S(1)}, u32[]{:S(2)}, u32[]{:S(2)}) collective-permute-start(f32[64,512]{1,0:T(8,128)S(1)} %add.96), channel_id=1, source_target_pairs={{0,16},{1,17},{2,0},{3,1},{4,20},{5,21},{6,4},{7,5},{8,24},{9,25},... | collective-permute-start | bytes 393224 | tf_op jit(solution)/shard_map/ppermute | solution.py:194
  58.5 4.0 %collective-permute-start.11 = (f32[64,512]{1,0:T(8,128)S(1)}, f32[64,512]{1,0:T(8,128)S(1)}, u32[]{:S(2)}, u32[]{:S(2)}) collective-permute-start(f32[64,512]{1,0:T(8,128)S(1)} %add.96), channel_id=1, source_target_pairs={{0,0},{1,1},{2,16},{3,17},{4,4},{5,5},{6,20},{7,21},{8,8},{9,9},{1... | collective-permute-start | bytes 393224 | tf_op jit(solution)/shard_map/ppermute | solution.py:194
  59.4 14.1 %collective-permute-start.16 = (f32[64,512]{1,0:T(8,128)S(1)}, f32[64,512]{1,0:T(8,128)S(1)}, u32[]{:S(2)}, u32[]{:S(2)}) collective-permute-start(f32[64,512]{1,0:T(8,128)S(1)} %add.99.refs_1_), channel_id=1, source_target_pairs={{0,4},{1,5},{2,6},{3,7},{4,0},{5,1},{6,2},{7,3},{8,12},{9,13},{10,... | collective-permute-start | bytes 393224 | tf_op jit(solution)/shard_map/ppermute | solution.py:194
  62.5 12.0 %collective-permute-start.15 = (f32[64,512]{1,0:T(8,128)S(1)}, f32[64,512]{1,0:T(8,128)S(1)}, u32[]{:S(2)}, u32[]{:S(2)}) collective-permute-start(f32[64,512]{1,0:T(8,128)S(1)} %add.97.refs_0_), channel_id=1, source_target_pairs={{0,4},{1,5},{2,6},{3,7},{4,0},{5,1},{6,2},{7,3},{8,12},{9,13},{10,... | collective-permute-start | bytes 393224 | tf_op jit(solution)/shard_map/ppermute | solution.py:194
  64.1 12.0 %collective-permute-start.18 = (f32[64,512]{1,0:T(8,128)S(1)}, f32[64,512]{1,0:T(8,128)S(1)}, u32[]{:S(2)}, u32[]{:S(2)}) collective-permute-start(f32[64,512]{1,0:T(8,128)S(1)} %add.99.refs_1_), channel_id=1, source_target_pairs={{0,8},{1,9},{2,10},{3,11},{4,12},{5,13},{6,14},{7,15},{8,0},{9,1},... | collective-permute-start | bytes 393224 | tf_op jit(solution)/shard_map/ppermute | solution.py:194
  70.0 7.2 %collective-permute-start.17 = (f32[64,512]{1,0:T(8,128)S(1)}, f32[64,512]{1,0:T(8,128)S(1)}, u32[]{:S(2)}, u32[]{:S(2)}) collective-permute-start(f32[64,512]{1,0:T(8,128)S(1)} %add.97.refs_0_), channel_id=1, source_target_pairs={{0,8},{1,9},{2,10},{3,11},{4,12},{5,13},{6,14},{7,15},{8,0},{9,1},... | collective-permute-start | bytes 393224 | tf_op jit(solution)/shard_map/ppermute | solution.py:194
  70.0 9.9 %collective-permute-start.20 = (f32[64,512]{1,0:T(8,128)S(1)}, f32[64,512]{1,0:T(8,128)S(1)}, u32[]{:S(2)}, u32[]{:S(2)}) collective-permute-start(f32[64,512]{1,0:T(8,128)S(1)} %add.99.refs_1_), channel_id=1, source_target_pairs={{0,12},{1,13},{2,14},{3,15},{4,8},{5,9},{6,10},{7,11},{8,4},{9,5},... | collective-permute-start | bytes 393224 | tf_op jit(solution)/shard_map/ppermute | solution.py:194
  73.5 8.8 %collective-permute-start.19 = (f32[64,512]{1,0:T(8,128)S(1)}, f32[64,512]{1,0:T(8,128)S(1)}, u32[]{:S(2)}, u32[]{:S(2)}) collective-permute-start(f32[64,512]{1,0:T(8,128)S(1)} %add.97.refs_0_), channel_id=1, source_target_pairs={{0,12},{1,13},{2,14},{3,15},{4,8},{5,9},{6,10},{7,11},{8,4},{9,5},... | collective-permute-start | bytes 393224 | tf_op jit(solution)/shard_map/ppermute | solution.py:194
  84.0 7.0 %collective-permute-start.21 = (f32[64,512]{1,0:T(8,128)S(1)}, f32[64,512]{1,0:T(8,128)S(1)}, u32[]{:S(2)}, u32[]{:S(2)}) collective-permute-start(f32[64,512]{1,0:T(8,128)S(1)} %get-tuple-element.154), channel_id=1, source_target_pairs={{0,1},{1,0},{2,3},{3,2},{4,5},{5,4},{6,7},{7,6},{8,9},{9,8},{10,11... | collective-permute-start | bytes 393224 | tf_op jit(solution)/shard_map/ppermute | solution.py:194
  84.6 9.6 %collective-permute-start.25 = (f32[64,512]{1,0:T(8,128)S(1)}, f32[64,512]{1,0:T(8,128)S(1)}, u32[]{:S(2)}, u32[]{:S(2)}) collective-permute-start(f32[64,512]{1,0:T(8,128)S(1)} %add.102), channel_id=1, source_target_pairs={{0,16},{1,17},{2,0},{3,1},{4,20},{5,21},{6,4},{7,5},{8,24},{9,25},... | collective-permute-start | bytes 393224 | tf_op jit(solution)/shard_map/ppermute | solution.py:194
  90.4 3.9 %collective-permute-start.26 = (f32[64,512]{1,0:T(8,128)S(1)}, f32[64,512]{1,0:T(8,128)S(1)}, u32[]{:S(2)}, u32[]{:S(2)}) collective-permute-start(f32[64,512]{1,0:T(8,128)S(1)} %add.102), channel_id=1, source_target_pairs={{0,0},{1,1},{2,16},{3,17},{4,4},{5,5},{6,20},{7,21},{8,8},{9,9},{1... | collective-permute-start | bytes 393224 | tf_op jit(solution)/shard_map/ppermute | solution.py:194
  91.1 6.3 %collective-permute-start.22 = (f32[64,512]{1,0:T(8,128)S(1)}, f32[64,512]{1,0:T(8,128)S(1)}, u32[]{:S(2)}, u32[]{:S(2)}) collective-permute-start(f32[64,512]{1,0:T(8,128)S(1)} %add.100), channel_id=1, source_target_pairs={{0,16},{1,17},{2,0},{3,1},{4,20},{5,21},{6,4},{7,5},{8,24},{9,25},... | collective-permute-start | bytes 393224 | tf_op jit(solution)/shard_map/ppermute | solution.py:194
  92.7 4.7 %collective-permute-start.23 = (f32[64,512]{1,0:T(8,128)S(1)}, f32[64,512]{1,0:T(8,128)S(1)}, u32[]{:S(2)}, u32[]{:S(2)}) collective-permute-start(f32[64,512]{1,0:T(8,128)S(1)} %add.100), channel_id=1, source_target_pairs={{0,0},{1,1},{2,16},{3,17},{4,4},{5,5},{6,20},{7,21},{8,8},{9,9},{1... | collective-permute-start | bytes 393224 | tf_op jit(solution)/shard_map/ppermute | solution.py:194
  94.3 14.1 %collective-permute-start.28 = (f32[64,512]{1,0:T(8,128)S(1)}, f32[64,512]{1,0:T(8,128)S(1)}, u32[]{:S(2)}, u32[]{:S(2)}) collective-permute-start(f32[64,512]{1,0:T(8,128)S(1)} %add_multiply_fusion.6.refs_1_), channel_id=1, source_target_pairs={{0,4},{1,5},{2,6},{3,7},{4,0},{5,1},{6,2},{7,3},{8,12},{9,13},{10,... | collective-permute-start | bytes 393224 | tf_op jit(solution)/shard_map/ppermute | solution.py:194
  97.4 12.0 %collective-permute-start.27 = (f32[64,512]{1,0:T(8,128)S(1)}, f32[64,512]{1,0:T(8,128)S(1)}, u32[]{:S(2)}, u32[]{:S(2)}) collective-permute-start(f32[64,512]{1,0:T(8,128)S(1)} %add_multiply_fusion.7.refs_0_), channel_id=1, source_target_pairs={{0,4},{1,5},{2,6},{3,7},{4,0},{5,1},{6,2},{7,3},{8,12},{9,13},{10,... | collective-permute-start | bytes 393224 | tf_op jit(solution)/shard_map/ppermute | solution.py:194
  99.0 12.0 %collective-permute-start.30 = (f32[64,512]{1,0:T(8,128)S(1)}, f32[64,512]{1,0:T(8,128)S(1)}, u32[]{:S(2)}, u32[]{:S(2)}) collective-permute-start(f32[64,512]{1,0:T(8,128)S(1)} %add_multiply_fusion.6.refs_1_), channel_id=1, source_target_pairs={{0,8},{1,9},{2,10},{3,11},{4,12},{5,13},{6,14},{7,15},{8,0},{9,1},... | collective-permute-start | bytes 393224 | tf_op jit(solution)/shard_map/ppermute | solution.py:194
  104.9 7.2 %collective-permute-start.29 = (f32[64,512]{1,0:T(8,128)S(1)}, f32[64,512]{1,0:T(8,128)S(1)}, u32[]{:S(2)}, u32[]{:S(2)}) collective-permute-start(f32[64,512]{1,0:T(8,128)S(1)} %add_multiply_fusion.7.refs_0_), channel_id=1, source_target_pairs={{0,8},{1,9},{2,10},{3,11},{4,12},{5,13},{6,14},{7,15},{8,0},{9,1},... | collective-permute-start | bytes 393224 | tf_op jit(solution)/shard_map/ppermute | solution.py:194
  104.9 9.9 %collective-permute-start.32 = (f32[64,512]{1,0:T(8,128)S(1)}, f32[64,512]{1,0:T(8,128)S(1)}, u32[]{:S(2)}, u32[]{:S(2)}) collective-permute-start(f32[64,512]{1,0:T(8,128)S(1)} %add_multiply_fusion.6.refs_1_), channel_id=1, source_target_pairs={{0,12},{1,13},{2,14},{3,15},{4,8},{5,9},{6,10},{7,11},{8,4},{9,5},... | collective-permute-start | bytes 393224 | tf_op jit(solution)/shard_map/ppermute | solution.py:194
  108.4 8.3 %collective-permute-start.31 = (f32[64,512]{1,0:T(8,128)S(1)}, f32[64,512]{1,0:T(8,128)S(1)}, u32[]{:S(2)}, u32[]{:S(2)}) collective-permute-start(f32[64,512]{1,0:T(8,128)S(1)} %add_multiply_fusion.7.refs_0_), channel_id=1, source_target_pairs={{0,12},{1,13},{2,14},{3,15},{4,8},{5,9},{6,10},{7,11},{8,4},{9,5},... | collective-permute-start | bytes 393224 | tf_op jit(solution)/shard_map/ppermute | solution.py:194
  118.4 7.5 %collective-permute-start.33 = (f32[64,512]{1,0:T(8,128)S(1)}, f32[64,512]{1,0:T(8,128)S(1)}, u32[]{:S(2)}, u32[]{:S(2)}) collective-permute-start(f32[64,512]{1,0:T(8,128)S(1)} %get-tuple-element.170), channel_id=1, source_target_pairs={{0,1},{1,0},{2,3},{3,2},{4,5},{5,4},{6,7},{7,6},{8,9},{9,8},{10,11... | collective-permute-start | bytes 393224 | tf_op jit(solution)/shard_map/ppermute | solution.py:194
  119.0 10.1 %collective-permute-start.37 = (f32[64,512]{1,0:T(8,128)S(1)}, f32[64,512]{1,0:T(8,128)S(1)}, u32[]{:S(2)}, u32[]{:S(2)}) collective-permute-start(f32[64,512]{1,0:T(8,128)S(1)} %add.106), channel_id=1, source_target_pairs={{0,16},{1,17},{2,0},{3,1},{4,20},{5,21},{6,4},{7,5},{8,24},{9,25},... | collective-permute-start | bytes 393224 | tf_op jit(solution)/shard_map/ppermute | solution.py:194
  125.3 3.9 %collective-permute-start.38 = (f32[64,512]{1,0:T(8,128)S(1)}, f32[64,512]{1,0:T(8,128)S(1)}, u32[]{:S(2)}, u32[]{:S(2)}) collective-permute-start(f32[64,512]{1,0:T(8,128)S(1)} %add.106), channel_id=1, source_target_pairs={{0,0},{1,1},{2,16},{3,17},{4,4},{5,5},{6,20},{7,21},{8,8},{9,9},{1... | collective-permute-start | bytes 393224 | tf_op jit(solution)/shard_map/ppermute | solution.py:194
  126.0 6.3 %collective-permute-start.34 = (f32[64,512]{1,0:T(8,128)S(1)}, f32[64,512]{1,0:T(8,128)S(1)}, u32[]{:S(2)}, u32[]{:S(2)}) collective-permute-start(f32[64,512]{1,0:T(8,128)S(1)} %add.104), channel_id=1, source_target_pairs={{0,16},{1,17},{2,0},{3,1},{4,20},{5,21},{6,4},{7,5},{8,24},{9,25},... | collective-permute-start | bytes 393224 | tf_op jit(solution)/shard_map/ppermute | solution.py:194
  127.3 4.9 %collective-permute-start.35 = (f32[64,512]{1,0:T(8,128)S(1)}, f32[64,512]{1,0:T(8,128)S(1)}, u32[]{:S(2)}, u32[]{:S(2)}) collective-permute-start(f32[64,512]{1,0:T(8,128)S(1)} %add.104), channel_id=1, source_target_pairs={{0,0},{1,1},{2,16},{3,17},{4,4},{5,5},{6,20},{7,21},{8,8},{9,9},{1... | collective-permute-start | bytes 393224 | tf_op jit(solution)/shard_map/ppermute | solution.py:194
  129.2 14.1 %collective-permute-start.40 = (f32[64,512]{1,0:T(8,128)S(1)}, f32[64,512]{1,0:T(8,128)S(1)}, u32[]{:S(2)}, u32[]{:S(2)}) collective-permute-start(f32[64,512]{1,0:T(8,128)S(1)} %add_multiply_fusion.4.refs_1_), channel_id=1, source_target_pairs={{0,4},{1,5},{2,6},{3,7},{4,0},{5,1},{6,2},{7,3},{8,12},{9,13},{10,... | collective-permute-start | bytes 393224 | tf_op jit(solution)/shard_map/ppermute | solution.py:194
  132.3 12.0 %collective-permute-start.39 = (f32[64,512]{1,0:T(8,128)S(1)}, f32[64,512]{1,0:T(8,128)S(1)}, u32[]{:S(2)}, u32[]{:S(2)}) collective-permute-start(f32[64,512]{1,0:T(8,128)S(1)} %add_multiply_fusion.5.refs_0_), channel_id=1, source_target_pairs={{0,4},{1,5},{2,6},{3,7},{4,0},{5,1},{6,2},{7,3},{8,12},{9,13},{10,... | collective-permute-start | bytes 393224 | tf_op jit(solution)/shard_map/ppermute | solution.py:194
  133.9 12.0 %collective-permute-start.42 = (f32[64,512]{1,0:T(8,128)S(1)}, f32[64,512]{1,0:T(8,128)S(1)}, u32[]{:S(2)}, u32[]{:S(2)}) collective-permute-start(f32[64,512]{1,0:T(8,128)S(1)} %add_multiply_fusion.4.refs_1_), channel_id=1, source_target_pairs={{0,8},{1,9},{2,10},{3,11},{4,12},{5,13},{6,14},{7,15},{8,0},{9,1},... | collective-permute-start | bytes 393224 | tf_op jit(solution)/shard_map/ppermute | solution.py:194
  139.8 7.2 %collective-permute-start.41 = (f32[64,512]{1,0:T(8,128)S(1)}, f32[64,512]{1,0:T(8,128)S(1)}, u32[]{:S(2)}, u32[]{:S(2)}) collective-permute-start(f32[64,512]{1,0:T(8,128)S(1)} %add_multiply_fusion.5.refs_0_), channel_id=1, source_target_pairs={{0,8},{1,9},{2,10},{3,11},{4,12},{5,13},{6,14},{7,15},{8,0},{9,1},... | collective-permute-start | bytes 393224 | tf_op jit(solution)/shard_map/ppermute | solution.py:194
  139.8 9.9 %collective-permute-start.44 = (f32[64,512]{1,0:T(8,128)S(1)}, f32[64,512]{1,0:T(8,128)S(1)}, u32[]{:S(2)}, u32[]{:S(2)}) collective-permute-start(f32[64,512]{1,0:T(8,128)S(1)} %add_multiply_fusion.4.refs_1_), channel_id=1, source_target_pairs={{0,12},{1,13},{2,14},{3,15},{4,8},{5,9},{6,10},{7,11},{8,4},{9,5},... | collective-permute-start | bytes 393224 | tf_op jit(solution)/shard_map/ppermute | solution.py:194
  143.3 8.3 %collective-permute-start.43 = (f32[64,512]{1,0:T(8,128)S(1)}, f32[64,512]{1,0:T(8,128)S(1)}, u32[]{:S(2)}, u32[]{:S(2)}) collective-permute-start(f32[64,512]{1,0:T(8,128)S(1)} %add_multiply_fusion.5.refs_0_), channel_id=1, source_target_pairs={{0,12},{1,13},{2,14},{3,15},{4,8},{5,9},{6,10},{7,11},{8,4},{9,5},... | collective-permute-start | bytes 393224 | tf_op jit(solution)/shard_map/ppermute | solution.py:194
  153.3 7.5 %collective-permute-start.45 = (f32[64,512]{1,0:T(8,128)S(1)}, f32[64,512]{1,0:T(8,128)S(1)}, u32[]{:S(2)}, u32[]{:S(2)}) collective-permute-start(f32[64,512]{1,0:T(8,128)S(1)} %get-tuple-element.186), channel_id=1, source_target_pairs={{0,1},{1,0},{2,3},{3,2},{4,5},{5,4},{6,7},{7,6},{8,9},{9,8},{10,11... | collective-permute-start | bytes 393224 | tf_op jit(solution)/shard_map/ppermute | solution.py:194
  153.9 10.1 %collective-permute-start.49 = (f32[64,512]{1,0:T(8,128)S(1)}, f32[64,512]{1,0:T(8,128)S(1)}, u32[]{:S(2)}, u32[]{:S(2)}) collective-permute-start(f32[64,512]{1,0:T(8,128)S(1)} %add.110), channel_id=1, source_target_pairs={{0,16},{1,17},{2,0},{3,1},{4,20},{5,21},{6,4},{7,5},{8,24},{9,25},... | collective-permute-start | bytes 393224 | tf_op jit(solution)/shard_map/ppermute | solution.py:194
  160.2 3.9 %collective-permute-start.50 = (f32[64,512]{1,0:T(8,128)S(1)}, f32[64,512]{1,0:T(8,128)S(1)}, u32[]{:S(2)}, u32[]{:S(2)}) collective-permute-start(f32[64,512]{1,0:T(8,128)S(1)} %add.110), channel_id=1, source_target_pairs={{0,0},{1,1},{2,16},{3,17},{4,4},{5,5},{6,20},{7,21},{8,8},{9,9},{1... | collective-permute-start | bytes 393224 | tf_op jit(solution)/shard_map/ppermute | solution.py:194
  160.9 6.3 %collective-permute-start.46 = (f32[64,512]{1,0:T(8,128)S(1)}, f32[64,512]{1,0:T(8,128)S(1)}, u32[]{:S(2)}, u32[]{:S(2)}) collective-permute-start(f32[64,512]{1,0:T(8,128)S(1)} %add.108), channel_id=1, source_target_pairs={{0,16},{1,17},{2,0},{3,1},{4,20},{5,21},{6,4},{7,5},{8,24},{9,25},... | collective-permute-start | bytes 393224 | tf_op jit(solution)/shard_map/ppermute | solution.py:194
  162.2 4.9 %collective-permute-start.47 = (f32[64,512]{1,0:T(8,128)S(1)}, f32[64,512]{1,0:T(8,128)S(1)}, u32[]{:S(2)}, u32[]{:S(2)}) collective-permute-start(f32[64,512]{1,0:T(8,128)S(1)} %add.108), channel_id=1, source_target_pairs={{0,0},{1,1},{2,16},{3,17},{4,4},{5,5},{6,20},{7,21},{8,8},{9,9},{1... | collective-permute-start | bytes 393224 | tf_op jit(solution)/shard_map/ppermute | solution.py:194
  164.1 14.1 %collective-permute-start.52 = (f32[64,512]{1,0:T(8,128)S(1)}, f32[64,512]{1,0:T(8,128)S(1)}, u32[]{:S(2)}, u32[]{:S(2)}) collective-permute-start(f32[64,512]{1,0:T(8,128)S(1)} %add_multiply_fusion.2.refs_1_), channel_id=1, source_target_pairs={{0,4},{1,5},{2,6},{3,7},{4,0},{5,1},{6,2},{7,3},{8,12},{9,13},{10,... | collective-permute-start | bytes 393224 | tf_op jit(solution)/shard_map/ppermute | solution.py:194
  167.2 12.0 %collective-permute-start.51 = (f32[64,512]{1,0:T(8,128)S(1)}, f32[64,512]{1,0:T(8,128)S(1)}, u32[]{:S(2)}, u32[]{:S(2)}) collective-permute-start(f32[64,512]{1,0:T(8,128)S(1)} %add_multiply_fusion.3.refs_0_), channel_id=1, source_target_pairs={{0,4},{1,5},{2,6},{3,7},{4,0},{5,1},{6,2},{7,3},{8,12},{9,13},{10,... | collective-permute-start | bytes 393224 | tf_op jit(solution)/shard_map/ppermute | solution.py:194
  168.7 12.0 %collective-permute-start.54 = (f32[64,512]{1,0:T(8,128)S(1)}, f32[64,512]{1,0:T(8,128)S(1)}, u32[]{:S(2)}, u32[]{:S(2)}) collective-permute-start(f32[64,512]{1,0:T(8,128)S(1)} %add_multiply_fusion.2.refs_1_), channel_id=1, source_target_pairs={{0,8},{1,9},{2,10},{3,11},{4,12},{5,13},{6,14},{7,15},{8,0},{9,1},... | collective-permute-start | bytes 393224 | tf_op jit(solution)/shard_map/ppermute | solution.py:194
  174.7 7.2 %collective-permute-start.53 = (f32[64,512]{1,0:T(8,128)S(1)}, f32[64,512]{1,0:T(8,128)S(1)}, u32[]{:S(2)}, u32[]{:S(2)}) collective-permute-start(f32[64,512]{1,0:T(8,128)S(1)} %add_multiply_fusion.3.refs_0_), channel_id=1, source_target_pairs={{0,8},{1,9},{2,10},{3,11},{4,12},{5,13},{6,14},{7,15},{8,0},{9,1},... | collective-permute-start | bytes 393224 | tf_op jit(solution)/shard_map/ppermute | solution.py:194
  174.7 9.9 %collective-permute-start.56 = (f32[64,512]{1,0:T(8,128)S(1)}, f32[64,512]{1,0:T(8,128)S(1)}, u32[]{:S(2)}, u32[]{:S(2)}) collective-permute-start(f32[64,512]{1,0:T(8,128)S(1)} %add_multiply_fusion.2.refs_1_), channel_id=1, source_target_pairs={{0,12},{1,13},{2,14},{3,15},{4,8},{5,9},{6,10},{7,11},{8,4},{9,5},... | collective-permute-start | bytes 393224 | tf_op jit(solution)/shard_map/ppermute | solution.py:194
  178.2 8.3 %collective-permute-start.55 = (f32[64,512]{1,0:T(8,128)S(1)}, f32[64,512]{1,0:T(8,128)S(1)}, u32[]{:S(2)}, u32[]{:S(2)}) collective-permute-start(f32[64,512]{1,0:T(8,128)S(1)} %add_multiply_fusion.3.refs_0_), channel_id=1, source_target_pairs={{0,12},{1,13},{2,14},{3,15},{4,8},{5,9},{6,10},{7,11},{8,4},{9,5},... | collective-permute-start | bytes 393224 | tf_op jit(solution)/shard_map/ppermute | solution.py:194
  188.2 7.5 %collective-permute-start.57 = (f32[64,512]{1,0:T(8,128)S(1)}, f32[64,512]{1,0:T(8,128)S(1)}, u32[]{:S(2)}, u32[]{:S(2)}) collective-permute-start(f32[64,512]{1,0:T(8,128)S(1)} %get-tuple-element.202), channel_id=1, source_target_pairs={{0,1},{1,0},{2,3},{3,2},{4,5},{5,4},{6,7},{7,6},{8,9},{9,8},{10,11... | collective-permute-start | bytes 393224 | tf_op jit(solution)/shard_map/ppermute | solution.py:194
  188.8 10.1 %collective-permute-start.61 = (f32[64,512]{1,0:T(8,128)S(1)}, f32[64,512]{1,0:T(8,128)S(1)}, u32[]{:S(2)}, u32[]{:S(2)}) collective-permute-start(f32[64,512]{1,0:T(8,128)S(1)} %add.114), channel_id=1, source_target_pairs={{0,16},{1,17},{2,0},{3,1},{4,20},{5,21},{6,4},{7,5},{8,24},{9,25},... | collective-permute-start | bytes 393224 | tf_op jit(solution)/shard_map/ppermute | solution.py:194
  195.1 3.9 %collective-permute-start.62 = (f32[64,512]{1,0:T(8,128)S(1)}, f32[64,512]{1,0:T(8,128)S(1)}, u32[]{:S(2)}, u32[]{:S(2)}) collective-permute-start(f32[64,512]{1,0:T(8,128)S(1)} %add.114), channel_id=1, source_target_pairs={{0,0},{1,1},{2,16},{3,17},{4,4},{5,5},{6,20},{7,21},{8,8},{9,9},{1... | collective-permute-start | bytes 393224 | tf_op jit(solution)/shard_map/ppermute | solution.py:194
  195.8 6.3 %collective-permute-start.58 = (f32[64,512]{1,0:T(8,128)S(1)}, f32[64,512]{1,0:T(8,128)S(1)}, u32[]{:S(2)}, u32[]{:S(2)}) collective-permute-start(f32[64,512]{1,0:T(8,128)S(1)} %add.112), channel_id=1, source_target_pairs={{0,16},{1,17},{2,0},{3,1},{4,20},{5,21},{6,4},{7,5},{8,24},{9,25},... | collective-permute-start | bytes 393224 | tf_op jit(solution)/shard_map/ppermute | solution.py:194
  197.1 4.9 %collective-permute-start.59 = (f32[64,512]{1,0:T(8,128)S(1)}, f32[64,512]{1,0:T(8,128)S(1)}, u32[]{:S(2)}, u32[]{:S(2)}) collective-permute-start(f32[64,512]{1,0:T(8,128)S(1)} %add.112), channel_id=1, source_target_pairs={{0,0},{1,1},{2,16},{3,17},{4,4},{5,5},{6,20},{7,21},{8,8},{9,9},{1... | collective-permute-start | bytes 393224 | tf_op jit(solution)/shard_map/ppermute | solution.py:194
  199.0 14.1 %collective-permute-start.64 = (f32[64,512]{1,0:T(8,128)S(1)}, f32[64,512]{1,0:T(8,128)S(1)}, u32[]{:S(2)}, u32[]{:S(2)}) collective-permute-start(f32[64,512]{1,0:T(8,128)S(1)} %get-tuple-element.226.refs_1_), channel_id=1, source_target_pairs={{0,4},{1,5},{2,6},{3,7},{4,0},{5,1},{6,2},{7,3},{8,12},{9,13},{10,... | collective-permute-start | bytes 393224 | tf_op jit(solution)/shard_map/ppermute | solution.py:194
  202.1 12.0 %collective-permute-start.63 = (f32[64,512]{1,0:T(8,128)S(1)}, f32[64,512]{1,0:T(8,128)S(1)}, u32[]{:S(2)}, u32[]{:S(2)}) collective-permute-start(f32[64,512]{1,0:T(8,128)S(1)} %get-tuple-element.228.refs_0_), channel_id=1, source_target_pairs={{0,4},{1,5},{2,6},{3,7},{4,0},{5,1},{6,2},{7,3},{8,12},{9,13},{10,... | collective-permute-start | bytes 393224 | tf_op jit(solution)/shard_map/ppermute | solution.py:194
  203.7 12.0 %collective-permute-start.66 = (f32[64,512]{1,0:T(8,128)S(1)}, f32[64,512]{1,0:T(8,128)S(1)}, u32[]{:S(2)}, u32[]{:S(2)}) collective-permute-start(f32[64,512]{1,0:T(8,128)S(1)} %get-tuple-element.226.refs_1_), channel_id=1, source_target_pairs={{0,8},{1,9},{2,10},{3,11},{4,12},{5,13},{6,14},{7,15},{8,0},{9,1},... | collective-permute-start | bytes 393224 | tf_op jit(solution)/shard_map/ppermute | solution.py:194
  209.6 7.2 %collective-permute-start.65 = (f32[64,512]{1,0:T(8,128)S(1)}, f32[64,512]{1,0:T(8,128)S(1)}, u32[]{:S(2)}, u32[]{:S(2)}) collective-permute-start(f32[64,512]{1,0:T(8,128)S(1)} %get-tuple-element.228.refs_0_), channel_id=1, source_target_pairs={{0,8},{1,9},{2,10},{3,11},{4,12},{5,13},{6,14},{7,15},{8,0},{9,1},... | collective-permute-start | bytes 393224 | tf_op jit(solution)/shard_map/ppermute | solution.py:194
  209.7 9.9 %collective-permute-start.68 = (f32[64,512]{1,0:T(8,128)S(1)}, f32[64,512]{1,0:T(8,128)S(1)}, u32[]{:S(2)}, u32[]{:S(2)}) collective-permute-start(f32[64,512]{1,0:T(8,128)S(1)} %get-tuple-element.226.refs_1_), channel_id=1, source_target_pairs={{0,12},{1,13},{2,14},{3,15},{4,8},{5,9},{6,10},{7,11},{8,4},{9,5},... | collective-permute-start | bytes 393224 | tf_op jit(solution)/shard_map/ppermute | solution.py:194
  213.1 8.3 %collective-permute-start.67 = (f32[64,512]{1,0:T(8,128)S(1)}, f32[64,512]{1,0:T(8,128)S(1)}, u32[]{:S(2)}, u32[]{:S(2)}) collective-permute-start(f32[64,512]{1,0:T(8,128)S(1)} %get-tuple-element.228.refs_0_), channel_id=1, source_target_pairs={{0,12},{1,13},{2,14},{3,15},{4,8},{5,9},{6,10},{7,11},{8,4},{9,5},... | collective-permute-start | bytes 393224 | tf_op jit(solution)/shard_map/ppermute | solution.py:194
  224.8 10.3 %collective-permute-start.70 = (f32[32,2048]{1,0:T(8,128)S(1)}, f32[32,2048]{1,0:T(8,128)S(1)}, u32[]{:S(2)}, u32[]{:S(2)}) collective-permute-start(f32[32,2048]{1,0:T(8,128)S(1)} %add.126), channel_id=1, source_target_pairs={{0,2},{1,3},{2,0},{3,1},{4,6},{5,7},{6,4},{7,5},{8,10},{9,11},{10,... | collective-permute-start | bytes 786440 | tf_op jit(solution)/shard_map/ppermute | solution.py:194
  (8 other events, 11.4 us)

commit v2 on v1

--- a/solution.py
+++ b/solution.py
@@ -12,7 +12,14 @@
 STEPS = 1
 AXES = ("row", "col", "rep")
 CHUNKS = 2
-RING = 12
+RING = 8
+
+
+def seat_order(fan, rep):
+    order = list(range(1, fan))
+    if rep % 2 and fan > 3:
+        order[0], order[1] = order[1], order[0]
+    return [0] + order
 
 
 def split_kernel(fan, parts, matrix, *refs):
@@ -30,7 +37,12 @@
     def copy(t):
         block = t % blocks
         row = pl.multiple_of(((rep ^ (block // each)) * each + block % each) * step, step)
-        column = pl.multiple_of(((seat ^ (t // blocks)) * parts + rep) * depth, depth)
+        even, odd = 0, 0
+        for q in range(fan):
+            even = jnp.where(t // blocks == q, seat_order(fan, 0)[q], even)
+            odd = jnp.where(t // blocks == q, seat_order(fan, 1)[q], odd)
+        other = seat ^ jnp.where(rep % 2 == 0, even, odd)
+        column = pl.multiple_of((other * parts + rep) * depth, depth)
         slot = t % slots
         return pltpu.make_async_copy(
             matrix.at[pl.ds(row, step), pl.ds(column, depth)], ring.at[slot], sems.at[slot]
@@ -48,15 +60,15 @@
             top = value.astype(jnp.bfloat16)
             rest = (value - top.astype(jnp.float32)).astype(jnp.bfloat16)
             column = pl.multiple_of(block * step, step)
-            for source, out in ((top, outs[2 * q]), (rest, outs[2 * q + 1])):
-                for at in range(0, depth, tile):
-                    turned = lax.dot_general(
-                        identity,
-                        source[:, at : at + tile],
-                        (((1,), (1,)), ((), ())),
-                        preferred_element_type=jnp.float32,
-                    )
-                    out[at : at + tile, pl.ds(column, step)] = turned.astype(jnp.bfloat16)
+            for at in range(0, depth, tile):
+                turned = lax.dot_general(
+                    identity,
+                    top[:, at : at + tile],
+                    (((1,), (1,)), ((), ())),
+                    preferred_element_type=jnp.float32,
+                )
+                outs[2 * q][at : at + tile, pl.ds(column, step)] = turned.astype(jnp.bfloat16)
+            outs[2 * q + 1][:, pl.ds(column, step)] = rest.T
 
             @pl.when(t + slots < total)
             def _():
@@ -75,7 +87,7 @@
             pltpu.VMEM((RING, step, depth), jnp.float32),
             pltpu.SemaphoreType.DMA((RING,)),
         ],
-        compiler_params=pltpu.CompilerParams(vmem_limit_bytes=20 << 20),
+        compiler_params=pltpu.CompilerParams(vmem_limit_bytes=14 << 20),
         cost_estimate=pl.CostEstimate(
             flops=8 * rows * depth * fan, bytes_accessed=4 * rows * depth * fan, transcendentals=0
         ),
@@ -84,38 +96,47 @@
     return list(zip(outs[::2], outs[1::2]))
 
 
-def product_kernel(ranges, chunks, first, *refs):
+def product_kernel(ranges, terms, first, *refs):
     refs = list(refs)
     before = None if first else [refs.pop(0) for _ in ranges]
-    value = jnp.concatenate([refs.pop(0)[...] for _ in range(chunks)], axis=1)
-    upper, lower = refs.pop(0), refs.pop(0)
-    count = value.shape[0]
-    high = value.astype(jnp.bfloat16)
-    low = (value - high.astype(jnp.float32)).astype(jnp.bfloat16)
-    both = jnp.concatenate([high, low], axis=0)
+    sides = []
+    for pieces, start in terms:
+        value = jnp.concatenate([refs.pop(0)[...] for _ in range(pieces)], axis=1)
+        high = value.astype(jnp.bfloat16)
+        low = (value - high.astype(jnp.float32)).astype(jnp.bfloat16)
+        both = jnp.concatenate([high, low], axis=0)
+        sides.append((high, both, slice(start, start + value.shape[1])))
+    weights = [(refs.pop(0), refs.pop(0)) for _ in terms]
     for place, (start, width) in enumerate(ranges):
         here = slice(start, start + width)
-        main = jnp.dot(both, upper[:, here], preferred_element_type=jnp.float32)
-        rest = jnp.dot(high, lower[:, here], preferred_element_type=jnp.float32)
-        total = main[:count] + (main[count:] + rest)
-        refs[place][...] = total if first else before[place][...] + total
-
-
-def product(before, pieces, weights, ranges):
-    count, depth = pieces[0].shape[0], weights[0].shape[0]
+        total = None if first else before[place][...]
+        for (high, both, rows), (upper, lower) in zip(sides, weights):
+            count = high.shape[0]
+            main = jnp.dot(both, upper[rows, here], preferred_element_type=jnp.float32)
+            rest = jnp.dot(high, lower[rows, here], preferred_element_type=jnp.float32)
+            value = main[:count] + (main[count:] + rest)
+            total = value if total is None else total + value
+        refs[place][...] = total
+
+
+def product(before, terms, ranges):
+    pieces = [piece for term in terms for piece in term[0]]
+    weights = [part for term in terms for part in term[2]]
+    count, chunk = pieces[0].shape
     width = sum(w for _, w in ranges)
-    operands = list(before or []) + list(pieces) + list(weights)
+    operands = list(before or []) + pieces + weights
     vmem = pl.BlockSpec(memory_space=pltpu.VMEM)
+    shapes = tuple((len(term[0]), term[1] * chunk) for term in terms)
     return pl.pallas_call(
-        functools.partial(product_kernel, ranges, len(pieces), before is None),
+        functools.partial(product_kernel, ranges, shapes, before is None),
         out_shape=tuple(jax.ShapeDtypeStruct((count, w), jnp.float32) for _, w in ranges),
         in_specs=[vmem] * len(operands),
         out_specs=(vmem,) * len(ranges),
         input_output_aliases={} if before is None else {i: i for i in range(len(ranges))},
-        compiler_params=pltpu.CompilerParams(vmem_limit_bytes=16 << 20),
+        compiler_params=pltpu.CompilerParams(vmem_limit_bytes=8 << 20),
         cost_estimate=pl.CostEstimate(
-            flops=6 * count * depth * width,
-            bytes_accessed=4 * depth * width,
+            flops=6 * count * chunk * len(pieces) * width,
+            bytes_accessed=4 * chunk * len(pieces) * width,
             transcendentals=0,
         ),
         name="product",
@@ -129,7 +150,7 @@
         out_shape=tuple(jax.ShapeDtypeStruct(shape, jnp.float32) for shape in outs),
         in_specs=[vmem] * len(operands),
         out_specs=(vmem,) * len(outs),
-        compiler_params=pltpu.CompilerParams(vmem_limit_bytes=16 << 20),
+        compiler_params=pltpu.CompilerParams(vmem_limit_bytes=8 << 20),
     )(*operands)
 
 
@@ -154,25 +175,23 @@
             out[p * size : (p + 1) * size, :] = value[:, h * width : (h + 1) * width]
 
 
-def close_kernel(fan, parts, chunks, scale, *refs):
-    count = parts * chunks
-    sums, running, outs = refs[:count], refs[count : count + chunks], refs[count + chunks :]
+def close_kernel(fan, parts, scale, *refs):
+    sums, running, outs = refs[:parts], refs[parts], refs[parts + 1 :]
     rep = lax.axis_index("rep")
     home = (lax.axis_index("row") // fan) == lax.axis_index("col")
-    size, width = outs[0].shape[0], running[0].shape[1]
+    size, width = outs[0].shape[0], running.shape[1]
     for p in range(parts):
-        for h in range(chunks):
-            for v in range(parts):
-                rows = slice(v * size, (v + 1) * size)
-                value = sums[p * chunks + h][rows, :] * scale
-                if p == 0:
-                    value = value + jnp.where(home, running[h][rows, :], 0.0)
-                at = pl.multiple_of((rep ^ p) * (width * chunks) + h * width, width)
-                for q in range(parts):
-
-                    @pl.when((rep ^ q) == v)
-                    def _(value=value, out=outs[q], at=at):
-                        out[:, pl.ds(at, width)] = value
+        for v in range(parts):
+            rows = slice(v * size, (v + 1) * size)
+            value = sums[p][rows, :] * scale
+            if p == 0:
+                value = value + jnp.where(home, running[rows, :], 0.0)
+            at = pl.multiple_of((rep ^ p) * width, width)
+            for q in range(parts):
+
+                @pl.when((rep ^ q) == v)
+                def _(value=value, out=outs[q], at=at):
+                    out[:, pl.ds(at, width)] = value
 
 
 def local(matrix, vectors):
@@ -203,7 +222,7 @@
         return move(value, lambda h, s, c, k: ((c - q) % cols, s, h, k))
 
     def swap_seat(value, q):
-        return move(value, lambda h, s, c, k: (h, s ^ q, c, k))
+        return move(value, lambda h, s, c, k: (h, s ^ seat_order(fan, k)[q], c, k))
 
     slots = list(whole_call(deal_kernel, [(size, depth)] * parts, vectors))
     slots = [slots[0]] + [swap_rep(slots[q], q) for q in range(1, parts)]
@@ -225,18 +244,16 @@
         groups = [own]
         for q in range(1, fan):
             groups.append([swap_seat(piece, q) for piece in own])
-        sums = None
-        for at in range(fan - 1):
-            sums = product(sums, groups[at], weights[at], ranges)
+        sums = product(None, [(own, 0, weights[0])], ranges)
+        for p in range(CHUNKS):
+            some = [([groups[q][p]], p, weights[q]) for q in range(1, fan)]
+            final = some.pop() if p == CHUNKS - 1 else None
+            if some:
+                sums = product(sums, some, ranges)
         last = [None] * len(ranges)
         for h in range(CHUNKS):
             places = range(h, len(ranges), CHUNKS)
-            done = product(
-                None if sums is None else [sums[i] for i in places],
-                groups[-1],
-                weights[-1],
-                tuple(ranges[i] for i in places),
-            )
+            done = product([sums[i] for i in places], [final], tuple(ranges[i] for i in places))
             for i, value in zip(places, done):
                 last[i] = value
         sums = last
@@ -248,20 +265,23 @@
                 for q in range(1, parts):
                     total = total + swap_rep(sums[q * CHUNKS + h], q)
                 pieces.append(total)
-    outs = whole_call(
-        functools.partial(close_kernel, fan, parts, CHUNKS, scale),
-        [(size, rows)] * parts,
-        *sums,
-        *running,
-    )
-    result = outs[0]
-    for q in range(1, parts):
-        result = result + swap_rep(outs[q], q)
-    q = 1
-    while q < cols:
-        result = result + swap_col(result, q)
-        q *= 2
-    return result
+    pieces = []
+    for h in range(CHUNKS):
+        outs = whole_call(
+            functools.partial(close_kernel, fan, parts, scale),
+            [(size, parts * width)] * parts,
+            *sums[h::CHUNKS],
+            running[h],
+        )
+        result = outs[0]
+        for q in range(1, parts):
+            result = result + swap_rep(outs[q], q)
+        q = 1
+        while q < cols:
+            result = result + swap_col(result, q)
+            q *= 2
+        pieces.append([result[:, p * width : (p + 1) * width] for p in range(parts)])
+    return jnp.concatenate([pieces[h][p] for p in range(parts) for h in range(CHUNKS)], axis=1)
 
 
 def solution(mesh):

time: 237 us -> 212 us (0.89)
  waiting for transfers between devices: 49 us -> 33.6 us
  starting transfers between devices: 130 us -> 124 us
  Pallas kernels: 54.1 us -> 50.9 us
    ppermute x71 -> x73, waiting for transfers between devices: 49 us -> 33.6 us  [move(): return lax.ppermute(value, AXES, pairs)]
    ppermute x71 -> x73, starting transfers between devices: 130 us -> 124 us  [move(): return lax.ppermute(value, AXES, pairs)]
    pallas_call x1, Pallas kernels: 16.9 us -> 13.1 us  [split_matrix(): pl.pallas_call(functools.partial(split_kernel, fan, parts), out_shape=(pl...]
  transfers between devices with their start and end apart: 71 -> 73, of which waited for: 32 -> 28; matrix products, arithmetic and copies ran while one was open for 0% -> 0% of each run, Pallas kernels for 20% -> 23%
where the time goes in v2:
time: 212 us
  starting transfers between devices  124 us (58%)
  Pallas kernels  50.9 us (24%)
  waiting for transfers between devices  33.6 us (16%)
    ppermute x73, starting transfers between devices, move(): return lax.ppermute(value, AXES, pairs)  124 us
    pallas_call x30, Pallas kernels, product(): pl.pallas_call(functools.partial(product_kernel, ranges, shapes, before i...  37.6 us
    ppermute x73, waiting for transfers between devices, move(): return lax.ppermute(value, AXES, pairs)  33.6 us
    pallas_call x1, Pallas kernels, split_matrix(): pl.pallas_call(functools.partial(split_kernel, fan, parts), out_shape=(pl...  13.1 us
  transfers between devices with their start and end apart: 73, of which 28 were waited for; matrix products, arithmetic and copies ran while one was open for 0% of the time, Pallas kernels for 23%

profile of v2, /device:TPU:0, one launch (start us, length us, event | category | flops | bytes accessed | tf_op | source)
XLA Modules:
  0.0 211.6 jit_solution(13755187234999811519)
XLA Ops:
  2.5 4.0 %collective-permute-start.1 = (f32[64,512]{1,0:T(8,128)S(1)}, f32[64,512]{1,0:T(8,128)S(1)}, u32[]{:S(2)}, u32[]{:S(2)}) collective-permute-start(f32[64,512]{1,0:T(8,128)S(1)} %get-tuple-element.119), channel_id=1, source_target_pairs={{0,16},{1,17},{2,0},{3,1},{4,20},{5,21},{6,4},{7,5},{8,24},{9,25},... | collective-permute-start | bytes 393224 | tf_op jit(solution)/shard_map/ppermute | solution.py:213
  6.5 1.5 collective-permute-start.2
  8.1 2.4 %collective-permute-done.1.refs_0_ = f32[64,512]{1,0:T(8,128)S(1)} collective-permute-done((f32[64,512]{1,0:T(8,128)S(1)}, f32[64,512]{1,0:T(8,128)S(1)}, u32[]{:S(2)}, u32[]{:S(2)}) %collective-permute-start.1) | collective-permute-done | bytes 131104 | tf_op jit(solution)/shard_map/ppermute | solution.py:213
  10.5 1.5 collective-permute-start.3
  12.0 6.3 %collective-permute-start.4 = (f32[64,512]{1,0:T(8,128)S(1)}, f32[64,512]{1,0:T(8,128)S(1)}, u32[]{:S(2)}, u32[]{:S(2)}) collective-permute-start(f32[64,512]{1,0:T(8,128)S(1)} %collective-permute-done.1.refs_0_), channel_id=1, source_target_pairs={{0,8},{1,5},{2,10},{3,7},{4,12},{5,1},{6,14},{7,3},{8,0},{9,13},{1... | collective-permute-start | bytes 393224 | tf_op jit(solution)/shard_map/ppermute | solution.py:213
  18.3 13.1 %split.1 = (bf16[1024,2048]{1,0:T(8,128)(2,1)S(1)}, bf16[1024,2048]{1,0:T(8,128)(2,1)S(1)}, bf16[1024,2048]{1,0:T(8,128)(2,1)S(1)}, bf16[1024,2048]{1,0:T(8,128)...) custom-call(f32[2048,8192]{1,0:T(8,128)} %matrix.1), custom_call_target="tpu_custom_call" | custom-call | flops 67108864 | bytes 33554432 | tf_op jit(solution)/shard_map/split/pallas_call | solution.py:81
  31.3 1.5 collective-permute-start.6
  32.9 2.0 collective-permute-start.7
  34.9 1.5 product.30
  36.5 2.3 %product.31 = (f32[64,512]{1,0:T(8,128)S(1)}, f32[64,512]{1,0:T(8,128)S(1)}, f32[64,512]{1,0:T(8,128)S(1)}, f32[64,512]{1,0:T(8,128)S(1)}) custom-call(f32[64,512]{1,0:T(8,128)S(1)} %get-tuple-element.123.refs_0_, f32[64,512]{1,0:T(8,128)S(1)} %get-tuple-element.124.refs_1_, ...), custom_call_target="tpu_custom_call", output_to_operand_aliasing={{0}: (0, {}), {1}: (1, {}), {2}: (2, {}), {3}: (3, {})} | custom-call | flops 1207959552 | bytes 12582912 | tf_op jit(solution)/shard_map/product/pallas_call | solution.py:130
  38.8 1.6 product.32
  40.3 2.0 collective-permute-done.8.refs_2_
  44.3 3.4 %collective-permute-start.10 = (f32[64,512]{1,0:T(8,128)S(1)}, f32[64,512]{1,0:T(8,128)S(1)}, u32[]{:S(2)}, u32[]{:S(2)}) collective-permute-start(f32[64,512]{1,0:T(8,128)S(1)} %add.102), channel_id=1, source_target_pairs={{0,16},{1,17},{2,0},{3,1},{4,20},{5,21},{6,4},{7,5},{8,24},{9,25},... | collective-permute-start | bytes 393224 | tf_op jit(solution)/shard_map/ppermute | solution.py:213
  48.4 2.3 %collective-permute-start.13 = (f32[64,512]{1,0:T(8,128)S(1)}, f32[64,512]{1,0:T(8,128)S(1)}, u32[]{:S(2)}, u32[]{:S(2)}) collective-permute-start(f32[64,512]{1,0:T(8,128)S(1)} %add.104), channel_id=1, source_target_pairs={{0,16},{1,17},{2,0},{3,1},{4,20},{5,21},{6,4},{7,5},{8,24},{9,25},... | collective-permute-start | bytes 393224 | tf_op jit(solution)/shard_map/ppermute | solution.py:213
  51.6 1.1 collective-permute-start.15
  52.7 5.8 %collective-permute-start.16 = (f32[64,512]{1,0:T(8,128)S(1)}, f32[64,512]{1,0:T(8,128)S(1)}, u32[]{:S(2)}, u32[]{:S(2)}) collective-permute-start(f32[64,512]{1,0:T(8,128)S(1)} %add.103.refs_0_), channel_id=1, source_target_pairs={{0,8},{1,5},{2,10},{3,7},{4,12},{5,1},{6,14},{7,3},{8,0},{9,13},{1... | collective-permute-start | bytes 393224 | tf_op jit(solution)/shard_map/ppermute | solution.py:213
  60.1 2.0 collective-permute-start.19
  62.1 1.5 product.35
  63.7 1.5 collective-permute-start.20
  65.1 3.5 %collective-permute-done.17.refs_6_ = f32[64,512]{1,0:T(8,128)S(1)} collective-permute-done((f32[64,512]{1,0:T(8,128)S(1)}, f32[64,512]{1,0:T(8,128)S(1)}, u32[]{:S(2)}, u32[]{:S(2)}) %collective-permute-start.17) | collective-permute-done | bytes 131104 | tf_op jit(solution)/shard_map/ppermute | solution.py:213
  68.7 2.2 %product.36 = (f32[64,512]{1,0:T(8,128)S(1)}, f32[64,512]{1,0:T(8,128)S(1)}, f32[64,512]{1,0:T(8,128)S(1)}, f32[64,512]{1,0:T(8,128)S(1)}) custom-call(f32[64,512]{1,0:T(8,128)S(1)} %get-tuple-element.145.refs_0_, f32[64,512]{1,0:T(8,128)S(1)} %get-tuple-element.146.refs_1_, ...), custom_call_target="tpu_custom_call", output_to_operand_aliasing={{0}: (0, {}), {1}: (1, {}), {2}: (2, {}), {3}: (3, {})} | custom-call | flops 1207959552 | bytes 12582912 | tf_op jit(solution)/shard_map/product/pallas_call | solution.py:130
  70.9 1.6 product.37
  74.8 3.6 %collective-permute-start.22 = (f32[64,512]{1,0:T(8,128)S(1)}, f32[64,512]{1,0:T(8,128)S(1)}, u32[]{:S(2)}, u32[]{:S(2)}) collective-permute-start(f32[64,512]{1,0:T(8,128)S(1)} %add.106), channel_id=1, source_target_pairs={{0,16},{1,17},{2,0},{3,1},{4,20},{5,21},{6,4},{7,5},{8,24},{9,25},... | collective-permute-start | bytes 393224 | tf_op jit(solution)/shard_map/ppermute | solution.py:213
  79.1 3.5 %collective-permute-start.25 = (f32[64,512]{1,0:T(8,128)S(1)}, f32[64,512]{1,0:T(8,128)S(1)}, u32[]{:S(2)}, u32[]{:S(2)}) collective-permute-start(f32[64,512]{1,0:T(8,128)S(1)} %add.108), channel_id=1, source_target_pairs={{0,16},{1,17},{2,0},{3,1},{4,20},{5,21},{6,4},{7,5},{8,24},{9,25},... | collective-permute-start | bytes 393224 | tf_op jit(solution)/shard_map/ppermute | solution.py:213
  83.7 6.1 %collective-permute-start.28 = (f32[64,512]{1,0:T(8,128)S(1)}, f32[64,512]{1,0:T(8,128)S(1)}, u32[]{:S(2)}, u32[]{:S(2)}) collective-permute-start(f32[64,512]{1,0:T(8,128)S(1)} %add_multiply_fusion.7.refs_0_), channel_id=1, source_target_pairs={{0,8},{1,5},{2,10},{3,7},{4,12},{5,1},{6,14},{7,3},{8,0},{9,13},{1... | collective-permute-start | bytes 393224 | tf_op jit(solution)/shard_map/ppermute | solution.py:213
  91.3 2.0 collective-permute-start.31
  93.3 1.5 product.40
  94.8 1.4 collective-permute-start.32
  97.2 2.6 %collective-permute-done.29.refs_6_ = f32[64,512]{1,0:T(8,128)S(1)} collective-permute-done((f32[64,512]{1,0:T(8,128)S(1)}, f32[64,512]{1,0:T(8,128)S(1)}, u32[]{:S(2)}, u32[]{:S(2)}) %collective-permute-start.29) | collective-permute-done | bytes 131104 | tf_op jit(solution)/shard_map/ppermute | solution.py:213
  99.9 2.3 %product.41 = (f32[64,512]{1,0:T(8,128)S(1)}, f32[64,512]{1,0:T(8,128)S(1)}, f32[64,512]{1,0:T(8,128)S(1)}, f32[64,512]{1,0:T(8,128)S(1)}) custom-call(f32[64,512]{1,0:T(8,128)S(1)} %get-tuple-element.161.refs_0_, f32[64,512]{1,0:T(8,128)S(1)} %get-tuple-element.162.refs_1_, ...), custom_call_target="tpu_custom_call", output_to_operand_aliasing={{0}: (0, {}), {1}: (1, {}), {2}: (2, {}), {3}: (3, {})} | custom-call | flops 1207959552 | bytes 12582912 | tf_op jit(solution)/shard_map/product/pallas_call | solution.py:130
  102.9 1.6 product.42
  106.4 3.5 %collective-permute-start.34 = (f32[64,512]{1,0:T(8,128)S(1)}, f32[64,512]{1,0:T(8,128)S(1)}, u32[]{:S(2)}, u32[]{:S(2)}) collective-permute-start(f32[64,512]{1,0:T(8,128)S(1)} %add.110), channel_id=1, source_target_pairs={{0,16},{1,17},{2,0},{3,1},{4,20},{5,21},{6,4},{7,5},{8,24},{9,25},... | collective-permute-start | bytes 393224 | tf_op jit(solution)/shard_map/ppermute | solution.py:213
  110.6 4.4 %collective-permute-start.37 = (f32[64,512]{1,0:T(8,128)S(1)}, f32[64,512]{1,0:T(8,128)S(1)}, u32[]{:S(2)}, u32[]{:S(2)}) collective-permute-start(f32[64,512]{1,0:T(8,128)S(1)} %add.112), channel_id=1, source_target_pairs={{0,16},{1,17},{2,0},{3,1},{4,20},{5,21},{6,4},{7,5},{8,24},{9,25},... | collective-permute-start | bytes 393224 | tf_op jit(solution)/shard_map/ppermute | solution.py:213
  116.2 5.0 %collective-permute-start.40 = (f32[64,512]{1,0:T(8,128)S(1)}, f32[64,512]{1,0:T(8,128)S(1)}, u32[]{:S(2)}, u32[]{:S(2)}) collective-permute-start(f32[64,512]{1,0:T(8,128)S(1)} %add_multiply_fusion.5.refs_0_), channel_id=1, source_target_pairs={{0,8},{1,5},{2,10},{3,7},{4,12},{5,1},{6,14},{7,3},{8,0},{9,13},{1... | collective-permute-start | bytes 393224 | tf_op jit(solution)/shard_map/ppermute | solution.py:213
  122.8 2.0 collective-permute-start.43
  124.8 1.5 product.45
  126.3 2.1 %collective-permute-start.44 = (f32[64,512]{1,0:T(8,128)S(1)}, f32[64,512]{1,0:T(8,128)S(1)}, u32[]{:S(2)}, u32[]{:S(2)}) collective-permute-start(f32[64,512]{1,0:T(8,128)S(1)} %add_multiply_fusion.4.refs_1_), channel_id=1, source_target_pairs={{0,12},{1,13},{2,14},{3,15},{4,8},{5,9},{6,10},{7,11},{8,4},{9,5},... | collective-permute-start | bytes 393224 | tf_op jit(solution)/shard_map/ppermute | solution.py:213
  128.7 3.3 %collective-permute-done.41.refs_6_ = f32[64,512]{1,0:T(8,128)S(1)} collective-permute-done((f32[64,512]{1,0:T(8,128)S(1)}, f32[64,512]{1,0:T(8,128)S(1)}, u32[]{:S(2)}, u32[]{:S(2)}) %collective-permute-start.41) | collective-permute-done | bytes 131104 | tf_op jit(solution)/shard_map/ppermute | solution.py:213
  131.9 2.2 %product.46 = (f32[64,512]{1,0:T(8,128)S(1)}, f32[64,512]{1,0:T(8,128)S(1)}, f32[64,512]{1,0:T(8,128)S(1)}, f32[64,512]{1,0:T(8,128)S(1)}) custom-call(f32[64,512]{1,0:T(8,128)S(1)} %get-tuple-element.177.refs_0_, f32[64,512]{1,0:T(8,128)S(1)} %get-tuple-element.178.refs_1_, ...), custom_call_target="tpu_custom_call", output_to_operand_aliasing={{0}: (0, {}), {1}: (1, {}), {2}: (2, {}), {3}: (3, {})} | custom-call | flops 1207959552 | bytes 12582912 | tf_op jit(solution)/shard_map/product/pallas_call | solution.py:130
  134.3 1.5 product.47
  138.3 3.0 %collective-permute-start.46 = (f32[64,512]{1,0:T(8,128)S(1)}, f32[64,512]{1,0:T(8,128)S(1)}, u32[]{:S(2)}, u32[]{:S(2)}) collective-permute-start(f32[64,512]{1,0:T(8,128)S(1)} %add.114), channel_id=1, source_target_pairs={{0,16},{1,17},{2,0},{3,1},{4,20},{5,21},{6,4},{7,5},{8,24},{9,25},... | collective-permute-start | bytes 393224 | tf_op jit(solution)/shard_map/ppermute | solution.py:213
  142.0 3.6 %collective-permute-start.49 = (f32[64,512]{1,0:T(8,128)S(1)}, f32[64,512]{1,0:T(8,128)S(1)}, u32[]{:S(2)}, u32[]{:S(2)}) collective-permute-start(f32[64,512]{1,0:T(8,128)S(1)} %add.116), channel_id=1, source_target_pairs={{0,16},{1,17},{2,0},{3,1},{4,20},{5,21},{6,4},{7,5},{8,24},{9,25},... | collective-permute-start | bytes 393224 | tf_op jit(solution)/shard_map/ppermute | solution.py:213
  146.3 1.1 collective-permute-start.51
  147.5 5.2 %collective-permute-start.52 = (f32[64,512]{1,0:T(8,128)S(1)}, f32[64,512]{1,0:T(8,128)S(1)}, u32[]{:S(2)}, u32[]{:S(2)}) collective-permute-start(f32[64,512]{1,0:T(8,128)S(1)} %add_multiply_fusion.3.refs_0_), channel_id=1, source_target_pairs={{0,8},{1,5},{2,10},{3,7},{4,12},{5,1},{6,14},{7,3},{8,0},{9,13},{1... | collective-permute-start | bytes 393224 | tf_op jit(solution)/shard_map/ppermute | solution.py:213
  154.2 2.0 collective-permute-start.55
  156.2 1.5 product.50
  157.7 2.0 collective-permute-start.56
  160.1 3.3 %collective-permute-done.53.refs_6_ = f32[64,512]{1,0:T(8,128)S(1)} collective-permute-done((f32[64,512]{1,0:T(8,128)S(1)}, f32[64,512]{1,0:T(8,128)S(1)}, u32[]{:S(2)}, u32[]{:S(2)}) %collective-permute-start.53) | collective-permute-done | bytes 131104 | tf_op jit(solution)/shard_map/ppermute | solution.py:213
  163.4 2.2 %product.51 = (f32[64,512]{1,0:T(8,128)S(1)}, f32[64,512]{1,0:T(8,128)S(1)}, f32[64,512]{1,0:T(8,128)S(1)}, f32[64,512]{1,0:T(8,128)S(1)}) custom-call(f32[64,512]{1,0:T(8,128)S(1)} %get-tuple-element.193.refs_0_, f32[64,512]{1,0:T(8,128)S(1)} %get-tuple-element.194.refs_1_, ...), custom_call_target="tpu_custom_call", output_to_operand_aliasing={{0}: (0, {}), {1}: (1, {}), {2}: (2, {}), {3}: (3, {})} | custom-call | flops 1207959552 | bytes 12582912 | tf_op jit(solution)/shard_map/product/pallas_call | solution.py:130
  165.7 1.6 product.52
  169.7 3.0 %collective-permute-start.58 = (f32[64,512]{1,0:T(8,128)S(1)}, f32[64,512]{1,0:T(8,128)S(1)}, u32[]{:S(2)}, u32[]{:S(2)}) collective-permute-start(f32[64,512]{1,0:T(8,128)S(1)} %add.118), channel_id=1, source_target_pairs={{0,16},{1,17},{2,0},{3,1},{4,20},{5,21},{6,4},{7,5},{8,24},{9,25},... | collective-permute-start | bytes 393224 | tf_op jit(solution)/shard_map/ppermute | solution.py:213
  173.4 3.6 %collective-permute-start.61 = (f32[64,512]{1,0:T(8,128)S(1)}, f32[64,512]{1,0:T(8,128)S(1)}, u32[]{:S(2)}, u32[]{:S(2)}) collective-permute-start(f32[64,512]{1,0:T(8,128)S(1)} %add.120), channel_id=1, source_target_pairs={{0,16},{1,17},{2,0},{3,1},{4,20},{5,21},{6,4},{7,5},{8,24},{9,25},... | collective-permute-start | bytes 393224 | tf_op jit(solution)/shard_map/ppermute | solution.py:213
  178.1 1.1 collective-permute-start.63
  179.2 4.9 %collective-permute-start.64 = (f32[64,512]{1,0:T(8,128)S(1)}, f32[64,512]{1,0:T(8,128)S(1)}, u32[]{:S(2)}, u32[]{:S(2)}) collective-permute-start(f32[64,512]{1,0:T(8,128)S(1)} %get-tuple-element.230.refs_0_), channel_id=1, source_target_pairs={{0,8},{1,5},{2,10},{3,7},{4,12},{5,1},{6,14},{7,3},{8,0},{9,13},{1... | collective-permute-start | bytes 393224 | tf_op jit(solution)/shard_map/ppermute | solution.py:213
  184.6 1.1 collective-permute-start.66
  185.7 2.0 collective-permute-start.67
  187.7 1.5 product.55
  189.2 2.0 collective-permute-start.68
  191.5 3.3 %collective-permute-done.65.refs_6_ = f32[64,512]{1,0:T(8,128)S(1)} collective-permute-done((f32[64,512]{1,0:T(8,128)S(1)}, f32[64,512]{1,0:T(8,128)S(1)}, u32[]{:S(2)}, u32[]{:S(2)}) %collective-permute-start.65) | collective-permute-done | bytes 131104 | tf_op jit(solution)/shard_map/ppermute | solution.py:213
  194.8 2.2 %product.56 = (f32[64,512]{1,0:T(8,128)S(1)}, f32[64,512]{1,0:T(8,128)S(1)}, f32[64,512]{1,0:T(8,128)S(1)}, f32[64,512]{1,0:T(8,128)S(1)}) custom-call(f32[64,512]{1,0:T(8,128)S(1)} %get-tuple-element.209.refs_0_, f32[64,512]{1,0:T(8,128)S(1)} %get-tuple-element.210.refs_1_, ...), custom_call_target="tpu_custom_call", output_to_operand_aliasing={{0}: (0, {}), {1}: (1, {}), {2}: (2, {}), {3}: (3, {})} | custom-call | flops 1207959552 | bytes 12582912 | tf_op jit(solution)/shard_map/product/pallas_call | solution.py:130
  197.1 1.6 product.57
  201.2 3.0 %collective-permute-start.70 = (f32[32,1024]{1,0:T(8,128)S(1)}, f32[32,1024]{1,0:T(8,128)S(1)}, u32[]{:S(2)}, u32[]{:S(2)}) collective-permute-start(f32[32,1024]{1,0:T(8,128)S(1)} %add.127), channel_id=1, source_target_pairs={{0,2},{1,3},{2,0},{3,1},{4,6},{5,7},{6,4},{7,5},{8,10},{9,11},{10,... | collective-permute-start | bytes 393224 | tf_op jit(solution)/shard_map/ppermute | solution.py:213
  205.0 3.5 %collective-permute-done.70 = f32[32,1024]{1,0:T(8,128)S(1)} collective-permute-done((f32[32,1024]{1,0:T(8,128)S(1)}, f32[32,1024]{1,0:T(8,128)S(1)}, u32[]{:S(2)}, u32[]{:S(2)}) %collective-permute-start.70) | collective-permute-done | bytes 131104 | tf_op jit(solution)/shard_map/ppermute | solution.py:213
  208.6 2.2 %collective-permute-done.72 = f32[32,1024]{1,0:T(8,128)S(1)} collective-permute-done((f32[32,1024]{1,0:T(8,128)S(1)}, f32[32,1024]{1,0:T(8,128)S(1)}, u32[]{:S(2)}, u32[]{:S(2)}) %collective-permute-start.72) | collective-permute-done | bytes 131104 | tf_op jit(solution)/shard_map/ppermute | solution.py:213
  (146 shorter events, 35.4 us)
Async XLA Ops:
  2.5 7.9 %collective-permute-start.1 = (f32[64,512]{1,0:T(8,128)S(1)}, f32[64,512]{1,0:T(8,128)S(1)}, u32[]{:S(2)}, u32[]{:S(2)}) collective-permute-start(f32[64,512]{1,0:T(8,128)S(1)} %get-tuple-element.119), channel_id=1, source_target_pairs={{0,16},{1,17},{2,0},{3,1},{4,20},{5,21},{6,4},{7,5},{8,24},{9,25},... | collective-permute-start | bytes 393224 | tf_op jit(solution)/shard_map/ppermute | solution.py:213
  6.5 24.8 %collective-permute-start.2 = (f32[64,512]{1,0:T(8,128)S(1)}, f32[64,512]{1,0:T(8,128)S(1)}, u32[]{:S(2)}, u32[]{:S(2)}) collective-permute-start(f32[64,512]{1,0:T(8,128)S(1)} %get-tuple-element.120), channel_id=1, source_target_pairs={{0,16},{1,17},{2,0},{3,1},{4,20},{5,21},{6,4},{7,5},{8,24},{9,25},... | collective-permute-start | bytes 393224 | tf_op jit(solution)/shard_map/ppermute | solution.py:213
  10.5 25.9 %collective-permute-start.3 = (f32[64,512]{1,0:T(8,128)S(1)}, f32[64,512]{1,0:T(8,128)S(1)}, u32[]{:S(2)}, u32[]{:S(2)}) collective-permute-start(f32[64,512]{1,0:T(8,128)S(1)} %collective-permute-done.1.refs_0_), channel_id=1, source_target_pairs={{0,4},{1,9},{2,6},{3,11},{4,0},{5,13},{6,2},{7,15},{8,12},{9,1},{1... | collective-permute-start | bytes 393224 | tf_op jit(solution)/shard_map/ppermute | solution.py:213
  12.0 24.5 %collective-permute-start.4 = (f32[64,512]{1,0:T(8,128)S(1)}, f32[64,512]{1,0:T(8,128)S(1)}, u32[]{:S(2)}, u32[]{:S(2)}) collective-permute-start(f32[64,512]{1,0:T(8,128)S(1)} %collective-permute-done.1.refs_0_), channel_id=1, source_target_pairs={{0,8},{1,5},{2,10},{3,7},{4,12},{5,1},{6,14},{7,3},{8,0},{9,13},{1... | collective-permute-start | bytes 393224 | tf_op jit(solution)/shard_map/ppermute | solution.py:213
  18.2 18.2 %collective-permute-start.5 = (f32[64,512]{1,0:T(8,128)S(1)}, f32[64,512]{1,0:T(8,128)S(1)}, u32[]{:S(2)}, u32[]{:S(2)}) collective-permute-start(f32[64,512]{1,0:T(8,128)S(1)} %collective-permute-done.1.refs_0_), channel_id=1, source_target_pairs={{0,12},{1,13},{2,14},{3,15},{4,8},{5,9},{6,10},{7,11},{8,4},{9,5},... | collective-permute-start | bytes 393224 | tf_op jit(solution)/shard_map/ppermute | solution.py:213
  31.3 7.4 %collective-permute-start.6 = (f32[64,512]{1,0:T(8,128)S(1)}, f32[64,512]{1,0:T(8,128)S(1)}, u32[]{:S(2)}, u32[]{:S(2)}) collective-permute-start(f32[64,512]{1,0:T(8,128)S(1)} %collective-permute-done.2.refs_1_), channel_id=1, source_target_pairs={{0,4},{1,9},{2,6},{3,11},{4,0},{5,13},{6,2},{7,15},{8,12},{9,1},{1... | collective-permute-start | bytes 393224 | tf_op jit(solution)/shard_map/ppermute | solution.py:213
  32.9 5.9 %collective-permute-start.7 = (f32[64,512]{1,0:T(8,128)S(1)}, f32[64,512]{1,0:T(8,128)S(1)}, u32[]{:S(2)}, u32[]{:S(2)}) collective-permute-start(f32[64,512]{1,0:T(8,128)S(1)} %collective-permute-done.2.refs_1_), channel_id=1, source_target_pairs={{0,8},{1,5},{2,10},{3,7},{4,12},{5,1},{6,14},{7,3},{8,0},{9,13},{1... | collective-permute-start | bytes 393224 | tf_op jit(solution)/shard_map/ppermute | solution.py:213
  36.4 5.9 %collective-permute-start.8 = (f32[64,512]{1,0:T(8,128)S(1)}, f32[64,512]{1,0:T(8,128)S(1)}, u32[]{:S(2)}, u32[]{:S(2)}) collective-permute-start(f32[64,512]{1,0:T(8,128)S(1)} %collective-permute-done.2.refs_1_), channel_id=1, source_target_pairs={{0,12},{1,13},{2,14},{3,15},{4,8},{5,9},{6,10},{7,11},{8,4},{9,5},... | collective-permute-start | bytes 393224 | tf_op jit(solution)/shard_map/ppermute | solution.py:213
  43.4 5.0 %collective-permute-start.12 = (f32[64,512]{1,0:T(8,128)S(1)}, f32[64,512]{1,0:T(8,128)S(1)}, u32[]{:S(2)}, u32[]{:S(2)}) collective-permute-start(f32[64,512]{1,0:T(8,128)S(1)} %get-tuple-element.144), channel_id=1, source_target_pairs={{0,1},{1,0},{2,3},{3,2},{4,5},{5,4},{6,7},{7,6},{8,9},{9,8},{10,11... | collective-permute-start | bytes 393224 | tf_op jit(solution)/shard_map/ppermute | solution.py:213
  44.3 7.3 %collective-permute-start.10 = (f32[64,512]{1,0:T(8,128)S(1)}, f32[64,512]{1,0:T(8,128)S(1)}, u32[]{:S(2)}, u32[]{:S(2)}) collective-permute-start(f32[64,512]{1,0:T(8,128)S(1)} %add.102), channel_id=1, source_target_pairs={{0,16},{1,17},{2,0},{3,1},{4,20},{5,21},{6,4},{7,5},{8,24},{9,25},... | collective-permute-start | bytes 393224 | tf_op jit(solution)/shard_map/ppermute | solution.py:213
  48.4 10.7 %collective-permute-start.13 = (f32[64,512]{1,0:T(8,128)S(1)}, f32[64,512]{1,0:T(8,128)S(1)}, u32[]{:S(2)}, u32[]{:S(2)}) collective-permute-start(f32[64,512]{1,0:T(8,128)S(1)} %add.104), channel_id=1, source_target_pairs={{0,16},{1,17},{2,0},{3,1},{4,20},{5,21},{6,4},{7,5},{8,24},{9,25},... | collective-permute-start | bytes 393224 | tf_op jit(solution)/shard_map/ppermute | solution.py:213
  50.7 8.4 %collective-permute-start.14 = (f32[64,512]{1,0:T(8,128)S(1)}, f32[64,512]{1,0:T(8,128)S(1)}, u32[]{:S(2)}, u32[]{:S(2)}) collective-permute-start(f32[64,512]{1,0:T(8,128)S(1)} %add.104), channel_id=1, source_target_pairs={{0,0},{1,1},{2,16},{3,17},{4,4},{5,5},{6,20},{7,21},{8,8},{9,9},{1... | collective-permute-start | bytes 393224 | tf_op jit(solution)/shard_map/ppermute | solution.py:213
  51.6 12.1 %collective-permute-start.15 = (f32[64,512]{1,0:T(8,128)S(1)}, f32[64,512]{1,0:T(8,128)S(1)}, u32[]{:S(2)}, u32[]{:S(2)}) collective-permute-start(f32[64,512]{1,0:T(8,128)S(1)} %add.103.refs_0_), channel_id=1, source_target_pairs={{0,4},{1,9},{2,6},{3,11},{4,0},{5,13},{6,2},{7,15},{8,12},{9,1},{1... | collective-permute-start | bytes 393224 | tf_op jit(solution)/shard_map/ppermute | solution.py:213
  52.7 12.4 %collective-permute-start.16 = (f32[64,512]{1,0:T(8,128)S(1)}, f32[64,512]{1,0:T(8,128)S(1)}, u32[]{:S(2)}, u32[]{:S(2)}) collective-permute-start(f32[64,512]{1,0:T(8,128)S(1)} %add.103.refs_0_), channel_id=1, source_target_pairs={{0,8},{1,5},{2,10},{3,7},{4,12},{5,1},{6,14},{7,3},{8,0},{9,13},{1... | collective-permute-start | bytes 393224 | tf_op jit(solution)/shard_map/ppermute | solution.py:213
  58.6 10.1 %collective-permute-start.17 = (f32[64,512]{1,0:T(8,128)S(1)}, f32[64,512]{1,0:T(8,128)S(1)}, u32[]{:S(2)}, u32[]{:S(2)}) collective-permute-start(f32[64,512]{1,0:T(8,128)S(1)} %add.103.refs_0_), channel_id=1, source_target_pairs={{0,12},{1,13},{2,14},{3,15},{4,8},{5,9},{6,10},{7,11},{8,4},{9,5},... | collective-permute-start | bytes 393224 | tf_op jit(solution)/shard_map/ppermute | solution.py:213
  59.1 11.8 %collective-permute-start.18 = (f32[64,512]{1,0:T(8,128)S(1)}, f32[64,512]{1,0:T(8,128)S(1)}, u32[]{:S(2)}, u32[]{:S(2)}) collective-permute-start(f32[64,512]{1,0:T(8,128)S(1)} %add.105.refs_1_), channel_id=1, source_target_pairs={{0,4},{1,9},{2,6},{3,11},{4,0},{5,13},{6,2},{7,15},{8,12},{9,1},{1... | collective-permute-start | bytes 393224 | tf_op jit(solution)/shard_map/ppermute | solution.py:213
  60.1 10.8 %collective-permute-start.19 = (f32[64,512]{1,0:T(8,128)S(1)}, f32[64,512]{1,0:T(8,128)S(1)}, u32[]{:S(2)}, u32[]{:S(2)}) collective-permute-start(f32[64,512]{1,0:T(8,128)S(1)} %add.105.refs_1_), channel_id=1, source_target_pairs={{0,8},{1,5},{2,10},{3,7},{4,12},{5,1},{6,14},{7,3},{8,0},{9,13},{1... | collective-permute-start | bytes 393224 | tf_op jit(solution)/shard_map/ppermute | solution.py:213
  63.7 9.2 %collective-permute-start.20 = (f32[64,512]{1,0:T(8,128)S(1)}, f32[64,512]{1,0:T(8,128)S(1)}, u32[]{:S(2)}, u32[]{:S(2)}) collective-permute-start(f32[64,512]{1,0:T(8,128)S(1)} %add.105.refs_1_), channel_id=1, source_target_pairs={{0,12},{1,13},{2,14},{3,15},{4,8},{5,9},{6,10},{7,11},{8,4},{9,5},... | collective-permute-start | bytes 393224 | tf_op jit(solution)/shard_map/ppermute | solution.py:213
  74.0 5.1 %collective-permute-start.24 = (f32[64,512]{1,0:T(8,128)S(1)}, f32[64,512]{1,0:T(8,128)S(1)}, u32[]{:S(2)}, u32[]{:S(2)}) collective-permute-start(f32[64,512]{1,0:T(8,128)S(1)} %get-tuple-element.160), channel_id=1, source_target_pairs={{0,1},{1,0},{2,3},{3,2},{4,5},{5,4},{6,7},{7,6},{8,9},{9,8},{10,11... | collective-permute-start | bytes 393224 | tf_op jit(solution)/shard_map/ppermute | solution.py:213
  74.8 8.5 %collective-permute-start.22 = (f32[64,512]{1,0:T(8,128)S(1)}, f32[64,512]{1,0:T(8,128)S(1)}, u32[]{:S(2)}, u32[]{:S(2)}) collective-permute-start(f32[64,512]{1,0:T(8,128)S(1)} %add.106), channel_id=1, source_target_pairs={{0,16},{1,17},{2,0},{3,1},{4,20},{5,21},{6,4},{7,5},{8,24},{9,25},... | collective-permute-start | bytes 393224 | tf_op jit(solution)/shard_map/ppermute | solution.py:213
  78.4 4.9 %collective-permute-start.23 = (f32[64,512]{1,0:T(8,128)S(1)}, f32[64,512]{1,0:T(8,128)S(1)}, u32[]{:S(2)}, u32[]{:S(2)}) collective-permute-start(f32[64,512]{1,0:T(8,128)S(1)} %add.106), channel_id=1, source_target_pairs={{0,0},{1,1},{2,16},{3,17},{4,4},{5,5},{6,20},{7,21},{8,8},{9,9},{1... | collective-permute-start | bytes 393224 | tf_op jit(solution)/shard_map/ppermute | solution.py:213
  79.1 11.1 %collective-permute-start.25 = (f32[64,512]{1,0:T(8,128)S(1)}, f32[64,512]{1,0:T(8,128)S(1)}, u32[]{:S(2)}, u32[]{:S(2)}) collective-permute-start(f32[64,512]{1,0:T(8,128)S(1)} %add.108), channel_id=1, source_target_pairs={{0,16},{1,17},{2,0},{3,1},{4,20},{5,21},{6,4},{7,5},{8,24},{9,25},... | collective-permute-start | bytes 393224 | tf_op jit(solution)/shard_map/ppermute | solution.py:213
  82.6 7.6 %collective-permute-start.26 = (f32[64,512]{1,0:T(8,128)S(1)}, f32[64,512]{1,0:T(8,128)S(1)}, u32[]{:S(2)}, u32[]{:S(2)}) collective-permute-start(f32[64,512]{1,0:T(8,128)S(1)} %add.108), channel_id=1, source_target_pairs={{0,0},{1,1},{2,16},{3,17},{4,4},{5,5},{6,20},{7,21},{8,8},{9,9},{1... | collective-permute-start | bytes 393224 | tf_op jit(solution)/shard_map/ppermute | solution.py:213
  83.3 11.5 %collective-permute-start.27 = (f32[64,512]{1,0:T(8,128)S(1)}, f32[64,512]{1,0:T(8,128)S(1)}, u32[]{:S(2)}, u32[]{:S(2)}) collective-permute-start(f32[64,512]{1,0:T(8,128)S(1)} %add_multiply_fusion.7.refs_0_), channel_id=1, source_target_pairs={{0,4},{1,9},{2,6},{3,11},{4,0},{5,13},{6,2},{7,15},{8,12},{9,1},{1... | collective-permute-start | bytes 393224 | tf_op jit(solution)/shard_map/ppermute | solution.py:213
  83.7 13.6 %collective-permute-start.28 = (f32[64,512]{1,0:T(8,128)S(1)}, f32[64,512]{1,0:T(8,128)S(1)}, u32[]{:S(2)}, u32[]{:S(2)}) collective-permute-start(f32[64,512]{1,0:T(8,128)S(1)} %add_multiply_fusion.7.refs_0_), channel_id=1, source_target_pairs={{0,8},{1,5},{2,10},{3,7},{4,12},{5,1},{6,14},{7,3},{8,0},{9,13},{1... | collective-permute-start | bytes 393224 | tf_op jit(solution)/shard_map/ppermute | solution.py:213
  89.7 10.1 %collective-permute-start.29 = (f32[64,512]{1,0:T(8,128)S(1)}, f32[64,512]{1,0:T(8,128)S(1)}, u32[]{:S(2)}, u32[]{:S(2)}) collective-permute-start(f32[64,512]{1,0:T(8,128)S(1)} %add_multiply_fusion.7.refs_0_), channel_id=1, source_target_pairs={{0,12},{1,13},{2,14},{3,15},{4,8},{5,9},{6,10},{7,11},{8,4},{9,5},... | collective-permute-start | bytes 393224 | tf_op jit(solution)/shard_map/ppermute | solution.py:213
  90.2 11.9 %collective-permute-start.30 = (f32[64,512]{1,0:T(8,128)S(1)}, f32[64,512]{1,0:T(8,128)S(1)}, u32[]{:S(2)}, u32[]{:S(2)}) collective-permute-start(f32[64,512]{1,0:T(8,128)S(1)} %add_multiply_fusion.6.refs_1_), channel_id=1, source_target_pairs={{0,4},{1,9},{2,6},{3,11},{4,0},{5,13},{6,2},{7,15},{8,12},{9,1},{1... | collective-permute-start | bytes 393224 | tf_op jit(solution)/shard_map/ppermute | solution.py:213
  91.3 11.6 %collective-permute-start.31 = (f32[64,512]{1,0:T(8,128)S(1)}, f32[64,512]{1,0:T(8,128)S(1)}, u32[]{:S(2)}, u32[]{:S(2)}) collective-permute-start(f32[64,512]{1,0:T(8,128)S(1)} %add_multiply_fusion.6.refs_1_), channel_id=1, source_target_pairs={{0,8},{1,5},{2,10},{3,7},{4,12},{5,1},{6,14},{7,3},{8,0},{9,13},{1... | collective-permute-start | bytes 393224 | tf_op jit(solution)/shard_map/ppermute | solution.py:213
  94.8 9.6 %collective-permute-start.32 = (f32[64,512]{1,0:T(8,128)S(1)}, f32[64,512]{1,0:T(8,128)S(1)}, u32[]{:S(2)}, u32[]{:S(2)}) collective-permute-start(f32[64,512]{1,0:T(8,128)S(1)} %add_multiply_fusion.6.refs_1_), channel_id=1, source_target_pairs={{0,12},{1,13},{2,14},{3,15},{4,8},{5,9},{6,10},{7,11},{8,4},{9,5},... | collective-permute-start | bytes 393224 | tf_op jit(solution)/shard_map/ppermute | solution.py:213
  105.5 5.0 %collective-permute-start.36 = (f32[64,512]{1,0:T(8,128)S(1)}, f32[64,512]{1,0:T(8,128)S(1)}, u32[]{:S(2)}, u32[]{:S(2)}) collective-permute-start(f32[64,512]{1,0:T(8,128)S(1)} %get-tuple-element.176), channel_id=1, source_target_pairs={{0,1},{1,0},{2,3},{3,2},{4,5},{5,4},{6,7},{7,6},{8,9},{9,8},{10,11... | collective-permute-start | bytes 393224 | tf_op jit(solution)/shard_map/ppermute | solution.py:213
  106.4 9.5 %collective-permute-start.34 = (f32[64,512]{1,0:T(8,128)S(1)}, f32[64,512]{1,0:T(8,128)S(1)}, u32[]{:S(2)}, u32[]{:S(2)}) collective-permute-start(f32[64,512]{1,0:T(8,128)S(1)} %add.110), channel_id=1, source_target_pairs={{0,16},{1,17},{2,0},{3,1},{4,20},{5,21},{6,4},{7,5},{8,24},{9,25},... | collective-permute-start | bytes 393224 | tf_op jit(solution)/shard_map/ppermute | solution.py:213
  109.9 6.0 %collective-permute-start.35 = (f32[64,512]{1,0:T(8,128)S(1)}, f32[64,512]{1,0:T(8,128)S(1)}, u32[]{:S(2)}, u32[]{:S(2)}) collective-permute-start(f32[64,512]{1,0:T(8,128)S(1)} %add.110), channel_id=1, source_target_pairs={{0,0},{1,1},{2,16},{3,17},{4,4},{5,5},{6,20},{7,21},{8,8},{9,9},{1... | collective-permute-start | bytes 393224 | tf_op jit(solution)/shard_map/ppermute | solution.py:213
  110.6 11.1 %collective-permute-start.37 = (f32[64,512]{1,0:T(8,128)S(1)}, f32[64,512]{1,0:T(8,128)S(1)}, u32[]{:S(2)}, u32[]{:S(2)}) collective-permute-start(f32[64,512]{1,0:T(8,128)S(1)} %add.112), channel_id=1, source_target_pairs={{0,16},{1,17},{2,0},{3,1},{4,20},{5,21},{6,4},{7,5},{8,24},{9,25},... | collective-permute-start | bytes 393224 | tf_op jit(solution)/shard_map/ppermute | solution.py:213
  115.0 6.7 %collective-permute-start.38 = (f32[64,512]{1,0:T(8,128)S(1)}, f32[64,512]{1,0:T(8,128)S(1)}, u32[]{:S(2)}, u32[]{:S(2)}) collective-permute-start(f32[64,512]{1,0:T(8,128)S(1)} %add.112), channel_id=1, source_target_pairs={{0,0},{1,1},{2,16},{3,17},{4,4},{5,5},{6,20},{7,21},{8,8},{9,9},{1... | collective-permute-start | bytes 393224 | tf_op jit(solution)/shard_map/ppermute | solution.py:213
  115.9 10.4 %collective-permute-start.39 = (f32[64,512]{1,0:T(8,128)S(1)}, f32[64,512]{1,0:T(8,128)S(1)}, u32[]{:S(2)}, u32[]{:S(2)}) collective-permute-start(f32[64,512]{1,0:T(8,128)S(1)} %add_multiply_fusion.5.refs_0_), channel_id=1, source_target_pairs={{0,4},{1,9},{2,6},{3,11},{4,0},{5,13},{6,2},{7,15},{8,12},{9,1},{1... | collective-permute-start | bytes 393224 | tf_op jit(solution)/shard_map/ppermute | solution.py:213
  116.2 12.5 %collective-permute-start.40 = (f32[64,512]{1,0:T(8,128)S(1)}, f32[64,512]{1,0:T(8,128)S(1)}, u32[]{:S(2)}, u32[]{:S(2)}) collective-permute-start(f32[64,512]{1,0:T(8,128)S(1)} %add_multiply_fusion.5.refs_0_), channel_id=1, source_target_pairs={{0,8},{1,5},{2,10},{3,7},{4,12},{5,1},{6,14},{7,3},{8,0},{9,13},{1... | collective-permute-start | bytes 393224 | tf_op jit(solution)/shard_map/ppermute | solution.py:213
  121.2 10.8 %collective-permute-start.41 = (f32[64,512]{1,0:T(8,128)S(1)}, f32[64,512]{1,0:T(8,128)S(1)}, u32[]{:S(2)}, u32[]{:S(2)}) collective-permute-start(f32[64,512]{1,0:T(8,128)S(1)} %add_multiply_fusion.5.refs_0_), channel_id=1, source_target_pairs={{0,12},{1,13},{2,14},{3,15},{4,8},{5,9},{6,10},{7,11},{8,4},{9,5},... | collective-permute-start | bytes 393224 | tf_op jit(solution)/shard_map/ppermute | solution.py:213
  121.7 12.5 %collective-permute-start.42 = (f32[64,512]{1,0:T(8,128)S(1)}, f32[64,512]{1,0:T(8,128)S(1)}, u32[]{:S(2)}, u32[]{:S(2)}) collective-permute-start(f32[64,512]{1,0:T(8,128)S(1)} %add_multiply_fusion.4.refs_1_), channel_id=1, source_target_pairs={{0,4},{1,9},{2,6},{3,11},{4,0},{5,13},{6,2},{7,15},{8,12},{9,1},{1... | collective-permute-start | bytes 393224 | tf_op jit(solution)/shard_map/ppermute | solution.py:213
  122.8 11.5 %collective-permute-start.43 = (f32[64,512]{1,0:T(8,128)S(1)}, f32[64,512]{1,0:T(8,128)S(1)}, u32[]{:S(2)}, u32[]{:S(2)}) collective-permute-start(f32[64,512]{1,0:T(8,128)S(1)} %add_multiply_fusion.4.refs_1_), channel_id=1, source_target_pairs={{0,8},{1,5},{2,10},{3,7},{4,12},{5,1},{6,14},{7,3},{8,0},{9,13},{1... | collective-permute-start | bytes 393224 | tf_op jit(solution)/shard_map/ppermute | solution.py:213
  126.3 10.1 %collective-permute-start.44 = (f32[64,512]{1,0:T(8,128)S(1)}, f32[64,512]{1,0:T(8,128)S(1)}, u32[]{:S(2)}, u32[]{:S(2)}) collective-permute-start(f32[64,512]{1,0:T(8,128)S(1)} %add_multiply_fusion.4.refs_1_), channel_id=1, source_target_pairs={{0,12},{1,13},{2,14},{3,15},{4,8},{5,9},{6,10},{7,11},{8,4},{9,5},... | collective-permute-start | bytes 393224 | tf_op jit(solution)/shard_map/ppermute | solution.py:213
  137.4 4.5 %collective-permute-start.48 = (f32[64,512]{1,0:T(8,128)S(1)}, f32[64,512]{1,0:T(8,128)S(1)}, u32[]{:S(2)}, u32[]{:S(2)}) collective-permute-start(f32[64,512]{1,0:T(8,128)S(1)} %get-tuple-element.192), channel_id=1, source_target_pairs={{0,1},{1,0},{2,3},{3,2},{4,5},{5,4},{6,7},{7,6},{8,9},{9,8},{10,11... | collective-permute-start | bytes 393224 | tf_op jit(solution)/shard_map/ppermute | solution.py:213
  138.3 8.0 %collective-permute-start.46 = (f32[64,512]{1,0:T(8,128)S(1)}, f32[64,512]{1,0:T(8,128)S(1)}, u32[]{:S(2)}, u32[]{:S(2)}) collective-permute-start(f32[64,512]{1,0:T(8,128)S(1)} %add.114), channel_id=1, source_target_pairs={{0,16},{1,17},{2,0},{3,1},{4,20},{5,21},{6,4},{7,5},{8,24},{9,25},... | collective-permute-start | bytes 393224 | tf_op jit(solution)/shard_map/ppermute | solution.py:213
  141.3 5.0 %collective-permute-start.47 = (f32[64,512]{1,0:T(8,128)S(1)}, f32[64,512]{1,0:T(8,128)S(1)}, u32[]{:S(2)}, u32[]{:S(2)}) collective-permute-start(f32[64,512]{1,0:T(8,128)S(1)} %add.114), channel_id=1, source_target_pairs={{0,0},{1,1},{2,16},{3,17},{4,4},{5,5},{6,20},{7,21},{8,8},{9,9},{1... | collective-permute-start | bytes 393224 | tf_op jit(solution)/shard_map/ppermute | solution.py:213
  142.0 11.1 %collective-permute-start.49 = (f32[64,512]{1,0:T(8,128)S(1)}, f32[64,512]{1,0:T(8,128)S(1)}, u32[]{:S(2)}, u32[]{:S(2)}) collective-permute-start(f32[64,512]{1,0:T(8,128)S(1)} %add.116), channel_id=1, source_target_pairs={{0,16},{1,17},{2,0},{3,1},{4,20},{5,21},{6,4},{7,5},{8,24},{9,25},... | collective-permute-start | bytes 393224 | tf_op jit(solution)/shard_map/ppermute | solution.py:213
  145.6 7.4 %collective-permute-start.50 = (f32[64,512]{1,0:T(8,128)S(1)}, f32[64,512]{1,0:T(8,128)S(1)}, u32[]{:S(2)}, u32[]{:S(2)}) collective-permute-start(f32[64,512]{1,0:T(8,128)S(1)} %add.116), channel_id=1, source_target_pairs={{0,0},{1,1},{2,16},{3,17},{4,4},{5,5},{6,20},{7,21},{8,8},{9,9},{1... | collective-permute-start | bytes 393224 | tf_op jit(solution)/shard_map/ppermute | solution.py:213
  146.3 11.3 %collective-permute-start.51 = (f32[64,512]{1,0:T(8,128)S(1)}, f32[64,512]{1,0:T(8,128)S(1)}, u32[]{:S(2)}, u32[]{:S(2)}) collective-permute-start(f32[64,512]{1,0:T(8,128)S(1)} %add_multiply_fusion.3.refs_0_), channel_id=1, source_target_pairs={{0,4},{1,9},{2,6},{3,11},{4,0},{5,13},{6,2},{7,15},{8,12},{9,1},{1... | collective-permute-start | bytes 393224 | tf_op jit(solution)/shard_map/ppermute | solution.py:213
  147.5 12.6 %collective-permute-start.52 = (f32[64,512]{1,0:T(8,128)S(1)}, f32[64,512]{1,0:T(8,128)S(1)}, u32[]{:S(2)}, u32[]{:S(2)}) collective-permute-start(f32[64,512]{1,0:T(8,128)S(1)} %add_multiply_fusion.3.refs_0_), channel_id=1, source_target_pairs={{0,8},{1,5},{2,10},{3,7},{4,12},{5,1},{6,14},{7,3},{8,0},{9,13},{1... | collective-permute-start | bytes 393224 | tf_op jit(solution)/shard_map/ppermute | solution.py:213
  152.6 10.8 %collective-permute-start.53 = (f32[64,512]{1,0:T(8,128)S(1)}, f32[64,512]{1,0:T(8,128)S(1)}, u32[]{:S(2)}, u32[]{:S(2)}) collective-permute-start(f32[64,512]{1,0:T(8,128)S(1)} %add_multiply_fusion.3.refs_0_), channel_id=1, source_target_pairs={{0,12},{1,13},{2,14},{3,15},{4,8},{5,9},{6,10},{7,11},{8,4},{9,5},... | collective-permute-start | bytes 393224 | tf_op jit(solution)/shard_map/ppermute | solution.py:213
  153.1 12.5 %collective-permute-start.54 = (f32[64,512]{1,0:T(8,128)S(1)}, f32[64,512]{1,0:T(8,128)S(1)}, u32[]{:S(2)}, u32[]{:S(2)}) collective-permute-start(f32[64,512]{1,0:T(8,128)S(1)} %add_multiply_fusion.2.refs_1_), channel_id=1, source_target_pairs={{0,4},{1,9},{2,6},{3,11},{4,0},{5,13},{6,2},{7,15},{8,12},{9,1},{1... | collective-permute-start | bytes 393224 | tf_op jit(solution)/shard_map/ppermute | solution.py:213
  154.2 11.5 %collective-permute-start.55 = (f32[64,512]{1,0:T(8,128)S(1)}, f32[64,512]{1,0:T(8,128)S(1)}, u32[]{:S(2)}, u32[]{:S(2)}) collective-permute-start(f32[64,512]{1,0:T(8,128)S(1)} %add_multiply_fusion.2.refs_1_), channel_id=1, source_target_pairs={{0,8},{1,5},{2,10},{3,7},{4,12},{5,1},{6,14},{7,3},{8,0},{9,13},{1... | collective-permute-start | bytes 393224 | tf_op jit(solution)/shard_map/ppermute | solution.py:213
  157.7 10.1 %collective-permute-start.56 = (f32[64,512]{1,0:T(8,128)S(1)}, f32[64,512]{1,0:T(8,128)S(1)}, u32[]{:S(2)}, u32[]{:S(2)}) collective-permute-start(f32[64,512]{1,0:T(8,128)S(1)} %add_multiply_fusion.2.refs_1_), channel_id=1, source_target_pairs={{0,12},{1,13},{2,14},{3,15},{4,8},{5,9},{6,10},{7,11},{8,4},{9,5},... | collective-permute-start | bytes 393224 | tf_op jit(solution)/shard_map/ppermute | solution.py:213
  168.8 4.5 %collective-permute-start.60 = (f32[64,512]{1,0:T(8,128)S(1)}, f32[64,512]{1,0:T(8,128)S(1)}, u32[]{:S(2)}, u32[]{:S(2)}) collective-permute-start(f32[64,512]{1,0:T(8,128)S(1)} %get-tuple-element.208), channel_id=1, source_target_pairs={{0,1},{1,0},{2,3},{3,2},{4,5},{5,4},{6,7},{7,6},{8,9},{9,8},{10,11... | collective-permute-start | bytes 393224 | tf_op jit(solution)/shard_map/ppermute | solution.py:213
  169.7 8.3 %collective-permute-start.58 = (f32[64,512]{1,0:T(8,128)S(1)}, f32[64,512]{1,0:T(8,128)S(1)}, u32[]{:S(2)}, u32[]{:S(2)}) collective-permute-start(f32[64,512]{1,0:T(8,128)S(1)} %add.118), channel_id=1, source_target_pairs={{0,16},{1,17},{2,0},{3,1},{4,20},{5,21},{6,4},{7,5},{8,24},{9,25},... | collective-permute-start | bytes 393224 | tf_op jit(solution)/shard_map/ppermute | solution.py:213
  172.7 5.3 %collective-permute-start.59 = (f32[64,512]{1,0:T(8,128)S(1)}, f32[64,512]{1,0:T(8,128)S(1)}, u32[]{:S(2)}, u32[]{:S(2)}) collective-permute-start(f32[64,512]{1,0:T(8,128)S(1)} %add.118), channel_id=1, source_target_pairs={{0,0},{1,1},{2,16},{3,17},{4,4},{5,5},{6,20},{7,21},{8,8},{9,9},{1... | collective-permute-start | bytes 393224 | tf_op jit(solution)/shard_map/ppermute | solution.py:213
  173.4 11.1 %collective-permute-start.61 = (f32[64,512]{1,0:T(8,128)S(1)}, f32[64,512]{1,0:T(8,128)S(1)}, u32[]{:S(2)}, u32[]{:S(2)}) collective-permute-start(f32[64,512]{1,0:T(8,128)S(1)} %add.120), channel_id=1, source_target_pairs={{0,16},{1,17},{2,0},{3,1},{4,20},{5,21},{6,4},{7,5},{8,24},{9,25},... | collective-permute-start | bytes 393224 | tf_op jit(solution)/shard_map/ppermute | solution.py:213
  177.0 7.5 %collective-permute-start.62 = (f32[64,512]{1,0:T(8,128)S(1)}, f32[64,512]{1,0:T(8,128)S(1)}, u32[]{:S(2)}, u32[]{:S(2)}) collective-permute-start(f32[64,512]{1,0:T(8,128)S(1)} %add.120), channel_id=1, source_target_pairs={{0,0},{1,1},{2,16},{3,17},{4,4},{5,5},{6,20},{7,21},{8,8},{9,9},{1... | collective-permute-start | bytes 393224 | tf_op jit(solution)/shard_map/ppermute | solution.py:213
  178.1 11.1 %collective-permute-start.63 = (f32[64,512]{1,0:T(8,128)S(1)}, f32[64,512]{1,0:T(8,128)S(1)}, u32[]{:S(2)}, u32[]{:S(2)}) collective-permute-start(f32[64,512]{1,0:T(8,128)S(1)} %get-tuple-element.230.refs_0_), channel_id=1, source_target_pairs={{0,4},{1,9},{2,6},{3,11},{4,0},{5,13},{6,2},{7,15},{8,12},{9,1},{1... | collective-permute-start | bytes 393224 | tf_op jit(solution)/shard_map/ppermute | solution.py:213
  179.2 12.3 %collective-permute-start.64 = (f32[64,512]{1,0:T(8,128)S(1)}, f32[64,512]{1,0:T(8,128)S(1)}, u32[]{:S(2)}, u32[]{:S(2)}) collective-permute-start(f32[64,512]{1,0:T(8,128)S(1)} %get-tuple-element.230.refs_0_), channel_id=1, source_target_pairs={{0,8},{1,5},{2,10},{3,7},{4,12},{5,1},{6,14},{7,3},{8,0},{9,13},{1... | collective-permute-start | bytes 393224 | tf_op jit(solution)/shard_map/ppermute | solution.py:213
  184.1 10.7 %collective-permute-start.65 = (f32[64,512]{1,0:T(8,128)S(1)}, f32[64,512]{1,0:T(8,128)S(1)}, u32[]{:S(2)}, u32[]{:S(2)}) collective-permute-start(f32[64,512]{1,0:T(8,128)S(1)} %get-tuple-element.230.refs_0_), channel_id=1, source_target_pairs={{0,12},{1,13},{2,14},{3,15},{4,8},{5,9},{6,10},{7,11},{8,4},{9,5},... | collective-permute-start | bytes 393224 | tf_op jit(solution)/shard_map/ppermute | solution.py:213
  184.6 12.4 %collective-permute-start.66 = (f32[64,512]{1,0:T(8,128)S(1)}, f32[64,512]{1,0:T(8,128)S(1)}, u32[]{:S(2)}, u32[]{:S(2)}) collective-permute-start(f32[64,512]{1,0:T(8,128)S(1)} %get-tuple-element.232.refs_1_), channel_id=1, source_target_pairs={{0,4},{1,9},{2,6},{3,11},{4,0},{5,13},{6,2},{7,15},{8,12},{9,1},{1... | collective-permute-start | bytes 393224 | tf_op jit(solution)/shard_map/ppermute | solution.py:213
  185.7 11.4 %collective-permute-start.67 = (f32[64,512]{1,0:T(8,128)S(1)}, f32[64,512]{1,0:T(8,128)S(1)}, u32[]{:S(2)}, u32[]{:S(2)}) collective-permute-start(f32[64,512]{1,0:T(8,128)S(1)} %get-tuple-element.232.refs_1_), channel_id=1, source_target_pairs={{0,8},{1,5},{2,10},{3,7},{4,12},{5,1},{6,14},{7,3},{8,0},{9,13},{1... | collective-permute-start | bytes 393224 | tf_op jit(solution)/shard_map/ppermute | solution.py:213
  189.2 10.0 %collective-permute-start.68 = (f32[64,512]{1,0:T(8,128)S(1)}, f32[64,512]{1,0:T(8,128)S(1)}, u32[]{:S(2)}, u32[]{:S(2)}) collective-permute-start(f32[64,512]{1,0:T(8,128)S(1)} %get-tuple-element.232.refs_1_), channel_id=1, source_target_pairs={{0,12},{1,13},{2,14},{3,15},{4,8},{5,9},{6,10},{7,11},{8,4},{9,5},... | collective-permute-start | bytes 393224 | tf_op jit(solution)/shard_map/ppermute | solution.py:213
  201.2 7.4 %collective-permute-start.70 = (f32[32,1024]{1,0:T(8,128)S(1)}, f32[32,1024]{1,0:T(8,128)S(1)}, u32[]{:S(2)}, u32[]{:S(2)}) collective-permute-start(f32[32,1024]{1,0:T(8,128)S(1)} %add.127), channel_id=1, source_target_pairs={{0,2},{1,3},{2,0},{3,1},{4,6},{5,7},{6,4},{7,5},{8,10},{9,11},{10,... | collective-permute-start | bytes 393224 | tf_op jit(solution)/shard_map/ppermute | solution.py:213
  204.3 6.6 %collective-permute-start.72 = (f32[32,1024]{1,0:T(8,128)S(1)}, f32[32,1024]{1,0:T(8,128)S(1)}, u32[]{:S(2)}, u32[]{:S(2)}) collective-permute-start(f32[32,1024]{1,0:T(8,128)S(1)} %add.134), channel_id=1, source_target_pairs={{0,2},{1,3},{2,0},{3,1},{4,6},{5,7},{6,4},{7,5},{8,10},{9,11},{10,... | collective-permute-start | bytes 393224 | tf_op jit(solution)/shard_map/ppermute | solution.py:213
  (10 other events, 18.6 us)
